TPU v7x, 128 devices: a whole 4x4x4 slice. The times are simulated.
128 devices in a mesh: inner: 16 (over z, y), fsdp: 8 (over x, core).
Axes of the slice: x: 4, y: 4, z: 4, core: 2. Of those that a mesh axis runs over, the one named last changes fastest.
Arguments:
- x_in: bfloat16 [65536, 1024], P(('inner', 'fsdp'))
- w_up: bfloat16 [3, 1024, 4096], P(None, ('inner', 'fsdp'))
- w_down: bfloat16 [3, 4096, 1024], P(None, ('inner', 'fsdp'))
- grad_out: bfloat16 [65536, 1024], P(('inner', 'fsdp'))
Outputs:
- output 1: bfloat16 [65536, 1024], P(('inner', 'fsdp'))
- output 2: bfloat16 [65536, 1024], P(('inner', 'fsdp'))
- output 3: float32 [3, 1024, 4096], P(None, ('inner', 'fsdp'))
- output 4: float32 [3, 4096, 1024], P(None, ('inner', 'fsdp'))
All inputs are finite; a program needn't handle non-finite values.
Results may differ from a plain program's by a relative error of at most 0.00768654.
Values are sent between devices in bfloat16 or wider.
A program may use at most 1 GiB of HBM per device.

v0:
```python
import jax
import jax.numpy as jnp
from jax import lax
from jax.sharding import PartitionSpec as P


def gelu_parts(pre_act):
    norm_cdf = 0.5 * (1.0 + lax.erf(pre_act * (2.0 ** -0.5)))
    norm_pdf = jnp.exp(-0.5 * pre_act * pre_act) * ((2.0 * jnp.pi) ** -0.5)
    return pre_act * norm_cdf, norm_cdf + pre_act * norm_pdf


def contract(left, right, left_dim, right_dim):
    return lax.dot_general(left, right, (((left_dim,), (right_dim,)), ((), ())), preferred_element_type=jnp.float32)


def layer_forward(x_cur, up_mat, down_mat):
    pre_act = contract(x_cur, up_mat, 1, 0)
    post_act = gelu_parts(pre_act)[0].astype(jnp.bfloat16)
    return (x_cur.astype(jnp.float32) + contract(post_act, down_mat, 1, 0)).astype(jnp.bfloat16)


def layer_backward(x_cur, g_cur, up_mat, down_mat):
    pre_act = contract(x_cur, up_mat, 1, 0)
    post_full, gelu_slope = gelu_parts(pre_act)
    post_act = post_full.astype(jnp.bfloat16)
    d_pre = (contract(g_cur, down_mat, 1, 1) * gelu_slope).astype(jnp.bfloat16)
    g_next = (g_cur.astype(jnp.float32) + contract(d_pre, up_mat, 1, 1)).astype(jnp.bfloat16)
    grad_up = contract(x_cur, d_pre, 0, 0)
    grad_down = contract(post_act, g_cur, 0, 0)
    return g_next, grad_up, grad_down


def solution(mesh):
    fsdp_size = mesh.shape["fsdp"]
    all_axes = ("inner", "fsdp")
    tok_spec = P(all_axes, None)
    weight_spec = P(None, all_axes, None)

    def device_step(x_loc, up_loc, down_loc, g_loc):
        layers = up_loc.shape[0]
        kept_layers = layers // 2
        copy_up_rows = up_loc.shape[1] * fsdp_size
        copy_down_rows = down_loc.shape[1] * fsdp_size
        inner_idx = lax.axis_index("inner")
        x_cur = x_loc
        layer_inputs = []
        copies = {}
        for layer in range(layers):
            full_up = lax.all_gather(up_loc[layer], all_axes, axis=0, tiled=True)
            full_down = lax.all_gather(down_loc[layer], all_axes, axis=0, tiled=True)
            layer_inputs.append(x_cur)
            x_cur = layer_forward(x_cur, full_up, full_down)
            if layer >= layers - kept_layers:
                copies[layer] = (
                    lax.dynamic_slice_in_dim(full_up, inner_idx * copy_up_rows, copy_up_rows, axis=0),
                    lax.dynamic_slice_in_dim(full_down, inner_idx * copy_down_rows, copy_down_rows, axis=0))
        g_cur = g_loc
        grads_up = [None] * layers
        grads_down = [None] * layers
        for layer in reversed(range(layers)):
            if layer in copies:
                full_up = lax.all_gather(copies[layer][0], "inner", axis=0, tiled=True)
                full_down = lax.all_gather(copies[layer][1], "inner", axis=0, tiled=True)
            else:
                full_up = lax.all_gather(up_loc[layer], all_axes, axis=0, tiled=True)
                full_down = lax.all_gather(down_loc[layer], all_axes, axis=0, tiled=True)
            g_cur, grad_up, grad_down = layer_backward(layer_inputs[layer], g_cur, full_up, full_down)
            grads_up[layer] = lax.psum_scatter(grad_up, all_axes, scatter_dimension=0, tiled=True)
            grads_down[layer] = lax.psum_scatter(grad_down, all_axes, scatter_dimension=0, tiled=True)
        return x_cur, g_cur, jnp.stack(grads_up), jnp.stack(grads_down)

    return jax.shard_map(device_step, mesh=mesh, in_specs=(tok_spec, weight_spec, weight_spec, tok_spec), out_specs=(tok_spec, tok_spec, weight_spec, weight_spec), check_vma=False)
```

profile of v0, /device:TPU:1, one launch (start us, length us, event | category | flops | bytes accessed | tf_op | source)
XLA Modules:
  0.0 4615.5 jit_solution(12749803755865613117)
XLA Ops:
  13.0 71.7 %all-gather.25.cloned.1.call-done = bf16[1,1024,4096]{2,1,0:T(8,128)(2,1)} async-done(((bf16[1,8,4096]{2,1,0:T(8,128)(2,1)}), bf16[1,1024,4096]{2,1,0:T(8,128)(2,1)}) %all-gather.25.cloned.1.call-update) | async-done | bytes 8388624 | tf_op jit(solution)/shard_map/all_gather | solution.py:50
  86.7 68.8 %all-gather.27.cloned.1.call-done = bf16[1,4096,1024]{2,1,0:T(8,128)(2,1)} async-done(((bf16[1,32,1024]{2,1,0:T(8,128)(2,1)}), bf16[1,4096,1024]{2,1,0:T(8,128)(2,1)}) %all-gather.27.cloned.1.call-update) | async-done | bytes 8388624 | tf_op jit(solution)/shard_map/all_gather | solution.py:51
  157.4 68.8 %all-gather.17.cloned.1.call-done = bf16[1,1024,4096]{2,1,0:T(8,128)(2,1)} async-done(((bf16[1,8,4096]{2,1,0:T(8,128)(2,1)}), bf16[1,1024,4096]{2,1,0:T(8,128)(2,1)}) %all-gather.17.cloned.1.call-update) | async-done | bytes 8388624 | tf_op jit(solution)/shard_map/all_gather | solution.py:50
  226.2 10.4 multiply_convert_fusion.3
  236.6 59.6 %all-gather.19.cloned.1.call-done = bf16[1,4096,1024]{2,1,0:T(8,128)(2,1)} async-done(((bf16[1,32,1024]{2,1,0:T(8,128)(2,1)}), bf16[1,4096,1024]{2,1,0:T(8,128)(2,1)}) %all-gather.19.cloned.1.call-update) | async-done | bytes 8388624 | tf_op jit(solution)/shard_map/all_gather | solution.py:51
  305.4 60.9 %all-gather.21.cloned.1.call-done = bf16[1,1024,4096]{2,1,0:T(8,128)(2,1)} async-done(((bf16[1,8,4096]{2,1,0:T(8,128)(2,1)}), bf16[1,1024,4096]{2,1,0:T(8,128)(2,1)}) %all-gather.21.cloned.1.call-update) | async-done | bytes 8388624 | tf_op jit(solution)/shard_map/all_gather | solution.py:50
  376.4 59.9 %all-gather.23.cloned.1.call-done = bf16[1,4096,1024]{2,1,0:T(8,128)(2,1)} async-done(((bf16[1,32,1024]{2,1,0:T(8,128)(2,1)}), bf16[1,4096,1024]{2,1,0:T(8,128)(2,1)}) %all-gather.23.cloned.1.call-update) | async-done | bytes 8388624 | tf_op jit(solution)/shard_map/all_gather | solution.py:51
  445.5 61.3 %all-gather.31.cloned.1.call-done = bf16[1,1024,4096]{2,1,0:T(8,128)(2,1)} async-done(((bf16[1,64,4096]{2,1,0:T(8,128)(2,1)}), bf16[1,1024,4096]{2,1,0:T(8,128)(2,1)}) %all-gather.31.cloned.1.call-update) | async-done | bytes 8388624 | tf_op jit(solution)/shard_map/all_gather | solution.py:63
  516.8 63.0 %all-gather.29.cloned.1.call-done = bf16[1,4096,1024]{2,1,0:T(8,128)(2,1)} async-done(((bf16[1,256,1024]{2,1,0:T(8,128)(2,1)}), bf16[1,4096,1024]{2,1,0:T(8,128)(2,1)}) %all-gather.29.cloned.1.call-update) | async-done | bytes 8388624 | tf_op jit(solution)/shard_map/all_gather | solution.py:64
  579.8 10.5 fusion.5
  610.0 10.5 fusion.11
  640.1 10.5 fusion.17
  660.7 17.4 copy.21
  679.3 10.3 fusion.48
  690.9 10.4 fusion.80
  702.5 10.6 fusion.79
  713.1 15.6 add_convert_fusion.3
  728.8 10.2 add_convert_fusion
  738.9 526.9 %reduce-scatter.23.cloned.1.call-done = f32[8,4096]{1,0:T(8,128)} async-done(((f32[1024,4096]{1,0:T(8,128)}), f32[8,4096]{1,0:T(8,128)}) %reduce-scatter.23.cloned.1.call-update) | async-done | bytes 131088
  1267.9 666.0 %reduce-scatter.21.cloned.1.call-done = f32[8,4096]{1,0:T(8,128)} async-done(((f32[1024,4096]{1,0:T(8,128)}), f32[8,4096]{1,0:T(8,128)}) %reduce-scatter.21.cloned.1.call-update) | async-done | bytes 131088
  1936.1 666.2 %reduce-scatter.19.cloned.1.call-done = f32[8,4096]{1,0:T(8,128)} async-done(((f32[1024,4096]{1,0:T(8,128)}), f32[8,4096]{1,0:T(8,128)}) %reduce-scatter.19.cloned.1.call-update) | async-done | bytes 131088
  2605.1 665.3 %reduce-scatter.17.cloned.1.call-done = f32[32,1024]{1,0:T(8,128)} async-done(((f32[4096,1024]{1,0:T(8,128)}), f32[32,1024]{1,0:T(8,128)}) %reduce-scatter.17.cloned.1.call-update) | async-done | bytes 131088 | tf_op jit(solution)/shard_map/reduce_scatter | solution.py:70
  3270.4 668.3 %reduce-scatter.15.cloned.1.call-done = f32[32,1024]{1,0:T(8,128)} async-done(((f32[4096,1024]{1,0:T(8,128)}), f32[32,1024]{1,0:T(8,128)}) %reduce-scatter.15.cloned.1.call-update) | async-done | bytes 131088 | tf_op jit(solution)/shard_map/reduce_scatter | solution.py:70
  3938.6 668.1 %reduce-scatter.13.cloned.1.call-done = f32[32,1024]{1,0:T(8,128)} async-done(((f32[4096,1024]{1,0:T(8,128)}), f32[32,1024]{1,0:T(8,128)}) %reduce-scatter.13.cloned.1.call-update) | async-done | bytes 131088 | tf_op jit(solution)/shard_map/reduce_scatter | solution.py:70
  (67 shorter events, 109.6 us)
Async XLA Ops:
  7.2 77.5 %all-gather.25.cloned.1.call-start = ((), (), s32[]{:S(2)}) async-start(), calls=%async_computation.13 | async-start | bytes 8454144 | tf_op jit(solution)/shard_map/all_gather | solution.py:50
  8.8 146.7 %all-gather.27.cloned.1.call-start = ((), (), s32[]{:S(2)}) async-start(), calls=%async_computation.14 | async-start | bytes 8454144 | tf_op jit(solution)/shard_map/all_gather | solution.py:51
  10.5 215.8 %all-gather.17.cloned.1.call-start = ((), (), s32[]{:S(2)}) async-start(), calls=%async_computation.9 | async-start | bytes 8454144 | tf_op jit(solution)/shard_map/all_gather | solution.py:50
  11.2 285.1 %all-gather.19.cloned.1.call-start = ((), (), s32[]{:S(2)}) async-start(), calls=%async_computation.10 | async-start | bytes 8454144 | tf_op jit(solution)/shard_map/all_gather | solution.py:51
  11.8 354.5 %all-gather.21.cloned.1.call-start = ((), (), s32[]{:S(2)}) async-start(), calls=%async_computation.11 | async-start | bytes 8454144 | tf_op jit(solution)/shard_map/all_gather | solution.py:50
  12.4 424.0 %all-gather.23.cloned.1.call-start = ((), (), s32[]{:S(2)}) async-start(), calls=%async_computation.12 | async-start | bytes 8454144 | tf_op jit(solution)/shard_map/all_gather | solution.py:51
  12.9 493.9 %all-gather.31.cloned.1.call-start = ((), (), s32[]{:S(2)}) async-start(), calls=%async_computation.16 | async-start | bytes 8912896 | tf_op jit(solution)/shard_map/all_gather | solution.py:63
  86.6 493.2 %all-gather.29.cloned.1.call-start = ((), (), s32[]{:S(2)}) async-start(), calls=%async_computation.15 | async-start | bytes 8912896 | tf_op jit(solution)/shard_map/all_gather | solution.py:64
  157.4 138.9 %copy-start.2 = (bf16[512,1024]{1,0:T(8,128)(2,1)S(1)}, bf16[512,1024]{1,0:T(8,128)(2,1)}, u32[]{:S(2)}) copy-start(bf16[512,1024]{1,0:T(8,128)(2,1)} %param.4) | copy-start | bytes 3145732
  157.4 1108.5 %reduce-scatter.23.cloned.1.call-start = ((), (), s32[]{:S(2)}) async-start(), calls=%async_computation.19 | async-start | bytes 16908288
  590.4 2.0 copy-start.1
  600.5 1333.4 %reduce-scatter.21.cloned.1.call-start = ((), (), s32[]{:S(2)}) async-start(), calls=%async_computation.18 | async-start | bytes 16908288
  610.0 10.6 copy-start.7
  620.5 2.0 copy-start
  630.7 1971.6 %reduce-scatter.19.cloned.1.call-start = ((), (), s32[]{:S(2)}) async-start(), calls=%async_computation.17 | async-start | bytes 16908288
  640.0 10.5 copy-start.5
  650.6 2.0 copy-start.4
  678.1 1.2 copy-start.3
  678.1 2592.2 %reduce-scatter.17.cloned.1.call-start = ((), (), s32[]{:S(2)}) async-start(), calls=%async_computation.8 | async-start | bytes 16908288 | tf_op jit(solution)/shard_map/reduce_scatter | solution.py:70
  689.7 1.2 copy-start.8
  689.7 3248.9 %reduce-scatter.15.cloned.1.call-start = ((), (), s32[]{:S(2)}) async-start(), calls=%async_computation.7 | async-start | bytes 16908288 | tf_op jit(solution)/shard_map/reduce_scatter | solution.py:70
  701.3 1.2 copy-start.6
  701.3 3905.4 %reduce-scatter.13.cloned.1.call-start = ((), (), s32[]{:S(2)}) async-start(), calls=%async_computation.6 | async-start | bytes 16908288 | tf_op jit(solution)/shard_map/reduce_scatter | solution.py:70
Sparse Core Ops, SparseCore 0:
  11.5 73.1 all-gather.24
  88.3 67.1 all-gather.26
  159.0 67.1 all-gather.16
  229.1 67.1 all-gather.18
  299.1 67.1 all-gather.20
  369.1 67.1 all-gather.22
  439.0 67.6 all-gather.30
  509.5 70.2 all-gather.28
  600.6 665.1 reduce-scatter.22
  1268.1 665.8 reduce-scatter.20
  1936.4 665.8 reduce-scatter.18
  2604.5 665.8 reduce-scatter.16
  3272.8 665.8 reduce-scatter.14
  3940.9 665.8 reduce-scatter.12
where the time goes:
time: 4630 us; the launch traced here: 4620 us
  waiting for transfers between devices  4380 us (95%)
  matrix products  181 us (4%)
    reduce_scatter x3, waiting for transfers between devices, device_step(): lax.psum_scatter(grad_down, all_axes, scatter_dimension=0, tiled=True)  2000 us
    unnamed x17, waiting for transfers between devices  1860 us
    all_gather x3, waiting for transfers between devices, device_step(): full_up = lax.all_gather(up_loc[layer], all_axes, axis=0, tiled=True)  201 us
    all_gather x3, waiting for transfers between devices, device_step(): full_down = lax.all_gather(down_loc[layer], all_axes, axis=0, tiled=True)  188 us
    dot_general x16, matrix products, contract(): lax.dot_general(left, right, (((left_dim,), (right_dim,)), ((), ())), pre...  164 us
  transfers between devices with their start and end apart: 14, of which 14 were waited for; matrix products, arithmetic and copies ran while one was open for 4% of the time, Pallas kernels for 0%

commit v1 on v0

v1 whole, which is shorter than its diff:
```python
import functools

import jax
import jax.numpy as jnp
from jax import lax
from jax.experimental import pallas as pl
from jax.experimental.pallas import tpu as pltpu
from jax.sharding import Mesh, PartitionSpec as P

CHIPS = ("z", "y", "x")
ALL = CHIPS + ("c",)
BF16 = jnp.bfloat16
F32 = jnp.float32
SIDE = 4
ROWS = 16
ORDERS = (("x", "y", "z"), ("y", "z", "x"), ("z", "x", "y"))


def gelu_parts(pre_act):
    norm_cdf = 0.5 * (1.0 + lax.erf(pre_act * (2.0 ** -0.5)))
    norm_pdf = jnp.exp(-0.5 * pre_act * pre_act) * ((2.0 * jnp.pi) ** -0.5)
    return pre_act * norm_cdf, norm_cdf + pre_act * norm_pdf


def swap(val):
    return lax.ppermute(val, "c", [(0, 1), (1, 0)])


def pair_rows(own, core):
    got = swap(own)
    return jnp.where(core == 0, jnp.concatenate([own, got], 0), jnp.concatenate([got, own], 0))


def dot(eq, left, right):
    return jnp.einsum(eq, left, right, preferred_element_type=F32)


def jobs_of(width):
    tile = width // 8
    cuts = ((0, 3 * tile), (3 * tile, 3 * tile), (6 * tile, 2 * tile))
    whole = [(mat, (0, width), ORDERS[mat]) for mat in range(3)]
    return whole + [(3, cuts[k], ORDERS[k]) for k in range(3)]


def view(ref, lead, axes, sel, cols=None):
    mid = tuple(sel.get(a, slice(None)) for a in axes)
    last = (slice(None), pl.ds(*cols)) if cols is not None else ()
    return ref.at[lead + mid + last]


def half(axis, k):
    return {axis: pl.ds(2 * k, 2)}


def ring_places():
    me = {a: lax.axis_index(a) for a in CHIPS}
    near = {a: [lax.rem(me[a] + d, SIDE) for d in range(SIDE)] for a in CHIPS}
    return me, near


def enter(near):
    barrier = pltpu.get_barrier_semaphore()
    for axis in CHIPS:
        for d in (1, 3):
            pl.semaphore_signal(barrier, inc=1, device_id={axis: near[axis][d]}, device_id_type=pl.DeviceIdType.MESH)
    pl.semaphore_wait(barrier, 6)


class Sender:
    def __init__(self, near, send_sem, recv_sem):
        self.near, self.send_sem, self.recv_sem, self.open = near, send_sem, recv_sem, {}

    def put(self, key, src, dst, axis, step):
        copy = pltpu.make_async_remote_copy(
            src_ref=src, dst_ref=dst, send_sem=self.send_sem.at[key], recv_sem=self.recv_sem.at[key],
            device_id={axis: self.near[axis][step]}, device_id_type=pl.DeviceIdType.MESH)
        copy.start()
        self.open[key] = copy

    def got(self, key):
        self.open[key].wait_recv()

    def close(self):
        for copy in self.open.values():
            copy.wait_send()


def gather_kernel(width, src, out, buf, send_sem, recv_sem, loc_sem, out_sem):
    me, near = ring_places()
    mine = {a: me[a] for a in CHIPS}
    jobs = jobs_of(width)
    first = pltpu.make_async_copy(src, view(buf, (slice(None),), CHIPS, mine), loc_sem.at[0])
    first.start()
    enter(near)
    first.wait()
    net = Sender(near, send_sem, recv_sem)
    for phase in range(3):
        def at(job, place, part=None):
            mat, cols, order = jobs[job]
            axis = order[2 - phase]
            sel = {a: me[a] for a in order[:2 - phase]}
            sel[axis] = place
            if part is not None:
                sel.update(half(order[3 - phase], part))
            return view(buf, (mat,), CHIPS, sel, cols)

        def push(job, slot, place, part, step):
            here = at(job, place, part)
            net.put((job, phase, slot), here, here, jobs[job][2][2 - phase], step)

        parts = (None,) if phase == 0 else (0, 1)
        for job in range(len(jobs)):
            places = near[jobs[job][2][2 - phase]]
            if phase == 0:
                push(job, 0, places[0], None, 1)
                push(job, 1, places[0], None, 3)
            else:
                push(job, 0, places[0], 0, 1)
                push(job, 1, places[0], 1, 3)
                push(job, 2, places[0], 1, 1)
                push(job, 3, places[0], 0, 3)
        for job in range(len(jobs)):
            places = near[jobs[job][2][2 - phase]]
            if phase == 0:
                net.got((job, 0, 0))
                push(job, 2, places[3], None, 1)
            else:
                net.got((job, phase, 0))
                push(job, 4, places[3], 0, 1)
                net.got((job, phase, 1))
                push(job, 5, places[1], 1, 3)
        for job in range(len(jobs)):
            for slot in ((1, 2) if phase == 0 else (2, 3, 4, 5)):
                net.got((job, phase, slot))
    last = [pltpu.make_async_copy(buf.at[mat], out.at[mat], out_sem.at[mat]) for mat in range(4)]
    for copy in last:
        copy.start()
    for copy in last:
        copy.wait()
    net.close()


def gather(packed, call_id):
    width = packed.shape[-1]
    full = (4, SIDE, SIDE, SIDE, ROWS, width)
    out = pl.pallas_call(
        functools.partial(gather_kernel, width),
        out_shape=jax.ShapeDtypeStruct(full, packed.dtype),
        in_specs=[pl.BlockSpec(memory_space=pl.ANY)],
        out_specs=pl.BlockSpec(memory_space=pl.ANY),
        scratch_shapes=[pltpu.VMEM(full, packed.dtype), pltpu.SemaphoreType.DMA((6, 3, 6)), pltpu.SemaphoreType.DMA((6, 3, 6)),
                        pltpu.SemaphoreType.DMA((1,)), pltpu.SemaphoreType.DMA((4,))],
        compiler_params=pltpu.CompilerParams(collective_id=call_id, has_side_effects=True),
        name="gather",
    )(packed)
    return out.reshape(4, SIDE ** 3 * ROWS, width)


def add_into(dst, src, lead):
    if not lead:
        dst[...] = dst[...] + src[...]
        return

    def step(k, _):
        add_into(dst.at[k], src.at[k], lead[1:])
        return 0

    lax.fori_loop(0, lead[0], step, 0)


def sum_kernel(width, up, down, out, buf, *rest):
    recv = rest[:18]
    send_sem, recv_sem, loc_sem = rest[18:]
    me, near = ring_places()
    jobs = jobs_of(width)
    net = Sender(near, send_sem, recv_sem)

    def take(mat):
        return (up if mat < 2 else down), mat % 2

    loads = {}
    for d in (2, 1, 3, 0):
        for job, (mat, cols, order) in enumerate(jobs):
            sel = {order[0]: near[order[0]][d]}
            ref, k = take(mat)
            loads[job, d] = pltpu.make_async_copy(view(ref, (k,), CHIPS, sel, cols), view(buf, (mat,), CHIPS, sel, cols),
                                                  loc_sem.at[job, d])
            loads[job, d].start()
    enter(near)
    for phase in range(3):
        def here(job, d, part=None):
            mat, cols, order = jobs[job]
            sel = {a: me[a] for a in order[:phase]}
            sel[order[phase]] = near[order[phase]][d]
            if part is not None:
                sel.update(half(order[phase + 1], part))
            return view(buf, (mat,), CHIPS, sel, cols)

        def there(job, slot, part=None):
            order = jobs[job][2]
            left = [a for a in CHIPS if a not in order[:phase + 1]]
            sel = {} if part is None else half(order[phase + 1], part)
            return view(recv[3 * job + phase], (slot,), left, sel)

        def lead(job, part=None):
            order = jobs[job][2]
            return [2 if part is not None and a == order[phase + 1] else SIDE for a in CHIPS if a not in order[:phase + 1]]

        def push(job, slot, d, part, to_slot, step):
            net.put((job, phase, slot), here(job, d, part), there(job, to_slot, part), jobs[job][2][phase], step)

        for job in range(len(jobs)):
            if phase == 0:
                loads[job, 2].wait()
            if phase == 2:
                push(job, 0, 2, None, 0, 1)
                push(job, 3, 3, None, 2, 3)
            else:
                push(job, 0, 2, 0, 0, 1)
                push(job, 1, 2, 1, 0, 3)
        for job in range(len(jobs)):
            if phase == 0:
                loads[job, 1].wait()
                loads[job, 3].wait()
            if phase < 2:
                push(job, 2, 1, 1, 1, 1)
                push(job, 3, 3, 0, 2, 3)
        for job in range(len(jobs)):
            net.got((job, phase, 0))
            if phase == 2:
                add_into(here(job, 1), there(job, 0), [])
                push(job, 2, 1, None, 1, 1)
            else:
                add_into(here(job, 1, 0), there(job, 0, 0), lead(job, 0))
                push(job, 4, 1, 0, 1, 1)
                net.got((job, phase, 1))
                add_into(here(job, 3, 1), there(job, 0, 1), lead(job, 1))
                push(job, 5, 3, 1, 2, 3)
        for job in range(len(jobs)):
            if phase == 0:
                loads[job, 0].wait()
            for slot in ((2, 3) if phase == 2 else (2, 3, 4, 5)):
                net.got((job, phase, slot))
            add_into(here(job, 0), there(job, 1), lead(job))
            add_into(here(job, 0), there(job, 2), lead(job))
    for mat in range(4):
        out[mat] = view(buf, (mat,), CHIPS, me)[...]
    net.close()


def scatter_sum(up, down, call_id):
    width = up.shape[-1]
    full = (SIDE, SIDE, SIDE, ROWS, width)
    blocks = []
    for mat, cols, order in jobs_of(width):
        blocks += [pltpu.VMEM((3,) + (SIDE,) * (2 - phase) + (ROWS, cols[1]), F32) for phase in range(3)]
    return pl.pallas_call(
        functools.partial(sum_kernel, width),
        out_shape=jax.ShapeDtypeStruct((4, ROWS, width), F32),
        in_specs=[pl.BlockSpec(memory_space=pl.ANY)] * 2,
        out_specs=pl.BlockSpec(memory_space=pltpu.VMEM),
        scratch_shapes=[pltpu.VMEM((4,) + full, F32)] + blocks
        + [pltpu.SemaphoreType.DMA((6, 3, 6)), pltpu.SemaphoreType.DMA((6, 3, 6)), pltpu.SemaphoreType.DMA((6, 4))],
        compiler_params=pltpu.CompilerParams(collective_id=call_id, has_side_effects=True),
        name="scatter_sum",
    )(up.reshape((2,) + full), down.reshape((2,) + full))


def pack_weights(up_loc, down_loc, core):
    layers, up_rows, hidden = up_loc.shape
    by_core = up_loc.reshape(layers, up_rows, 64, 2, 2, 16)
    mine = lax.dynamic_index_in_dim(by_core, core, 3, keepdims=False)
    other = lax.dynamic_index_in_dim(by_core, 1 - core, 3, keepdims=False)
    mine, other = (v.transpose(0, 3, 1, 2, 4).reshape(layers, 2, up_rows, hidden // 4) for v in (mine, other))
    got = swap(other)
    up = jnp.where(core == 0, jnp.concatenate([mine, got], 2), jnp.concatenate([got, mine], 2))
    return jnp.concatenate([up, down_loc.reshape(layers, 2, 16, -1)], 1)


def unpack_up_grad(grad, core):
    layers = grad.shape[0]
    rows = grad.reshape(layers, 2, 2, 8, 64, 16)
    mine = lax.dynamic_index_in_dim(rows, core, 2, keepdims=False)
    got = swap(lax.dynamic_index_in_dim(rows, 1 - core, 2, keepdims=False))
    both = jnp.where(core == 0, jnp.stack([mine, got]), jnp.stack([got, mine]))
    return both.transpose(1, 3, 4, 0, 2, 5).reshape(layers, 8, 4096)


def solution(mesh):
    grid = Mesh(mesh.devices.reshape(SIDE, SIDE, SIDE, 2), ALL)
    tok_spec = P(ALL, None)
    weight_spec = P(None, ALL, None)

    def device_step(x_loc, up_loc, down_loc, g_loc):
        layers = up_loc.shape[0]
        tokens = x_loc.shape[0]
        core = lax.axis_index("c")
        packed = pack_weights(up_loc, down_loc, core)
        x_cur = pair_rows(x_loc, core)
        g_cur = pair_rows(g_loc, core)
        saved = []
        for layer in range(layers):
            full = gather(packed[layer], layer)
            pre = [dot("tk,kn->tn", x_cur, full[j]) for j in range(2)]
            act = [gelu_parts(p)[0].astype(BF16) for p in pre]
            part = dot("tn,nm->tm", act[0], full[2]) + dot("tn,nm->tm", act[1], full[3])
            saved.append((x_cur, pre, act))
            x_cur = (x_cur.astype(F32) + (part + swap(part))).astype(BF16)
        y_out = lax.dynamic_slice_in_dim(x_cur, core * tokens, tokens, 0)
        mark = x_cur
        grads = [None] * layers
        for layer in reversed(range(layers)):
            again, _ = lax.optimization_barrier((packed[layer], mark))
            full = gather(again, layers + layer)
            x_in, pre, act = saved[layer]
            d_pre = [(dot("tm,nm->tn", g_cur, full[2 + j]) * gelu_parts(pre[j])[1]).astype(BF16) for j in range(2)]
            grad_down = jnp.stack([dot("tn,tm->nm", act[j], g_cur) for j in range(2)])
            grad_up = jnp.stack([dot("tk,tn->kn", x_in, d_pre[j]) for j in range(2)])
            part = dot("tn,kn->tk", d_pre[0], full[0]) + dot("tn,kn->tk", d_pre[1], full[1])
            g_cur = (g_cur.astype(F32) + (part + swap(part))).astype(BF16)
            grads[layer] = scatter_sum(grad_up, grad_down, 2 * layers + layer)
            mark = g_cur
        grads = jnp.stack(grads)
        grad_up = unpack_up_grad(grads[:, :2], core)
        grad_in = lax.dynamic_slice_in_dim(g_cur, core * tokens, tokens, 0)
        return y_out, grad_in, grad_up, grads[:, 2:].reshape(layers, 32, -1)

    return jax.shard_map(device_step, mesh=grid, in_specs=(tok_spec, weight_spec, weight_spec, tok_spec),
                         out_specs=(tok_spec, tok_spec, weight_spec, weight_spec), check_vma=False)
```

time: 4630 us -> 768 us (0.17)
  waiting for transfers between devices: 4380 us -> 7.23 us
  Pallas kernels: 0 us -> 463 us
    reduce_scatter x3 -> x0, waiting for transfers between devices: 2000 us -> none  [device_step(): lax.psum_scatter(grad_down, all_axes, scatter_dimension=0, tiled=True)]
    unnamed x17 -> x0, waiting for transfers between devices: 1860 us -> none
    all_gather x8 -> x0, waiting for transfers between devices: 514 us -> none  [the longest x3 201 us: device_step(): full_up = lax.all_gather(up_loc[layer], all_axes, axis=0, tiled=True)]
    pallas_call x0 -> x9, Pallas kernels: none -> 463 us  [the longest x6 253 us: gather(): pl.pallas_call(functools.partial(gather_kernel, width), out_shape=jax.Sha...]
    dot_general x16 -> x36, matrix products: 164 us -> 143 us  [dot(): return jnp.einsum(eq, left, right, preferred_element_type=F32)]
  transfers between devices with their start and end apart: 14 -> 10, of which waited for: 14 -> 2; matrix products, arithmetic and copies ran while one was open for 4% -> 16% of each run, Pallas kernels for 0% -> 50%
where the time goes in v1:
time: 768 us; the launch traced here: 763 us
  Pallas kernels  463 us (60%)
  matrix products  143 us (19%)
  local copies, waits for them, and re-layouts  56.5 us (7%)
  other arithmetic  48 us (6%)
  starting transfers between devices  43.1 us (6%)
    pallas_call x6, Pallas kernels, gather(): pl.pallas_call(functools.partial(gather_kernel, width), out_shape=jax.Sha...  253 us
    pallas_call x3, Pallas kernels, scatter_sum(): pl.pallas_call(functools.partial(sum_kernel, width), out_shape=jax.ShapeD...  210 us
    dot_general x36, matrix products, dot(): return jnp.einsum(eq, left, right, preferred_element_type=F32)  143 us
    ppermute x10, starting transfers between devices, swap(): return lax.ppermute(val, 'c', [(0, 1), (1, 0)])  43.1 us
    another operation x3, other arithmetic, device_step(): grad_up = jnp.stack([dot('tk,tn->kn', x_in, d_pre[j]) for j in range(2)])  20.6 us
  transfers between devices with their start and end apart: 10, of which 2 were waited for; matrix products, arithmetic and copies ran while one was open for 16% of the time, Pallas kernels for 50%

profile of v1, /device:TPU:1, one launch (start us, length us, event | category | flops | bytes accessed | tf_op | source)
XLA Modules:
  0.0 762.6 jit_solution(5549360741753909502)
XLA Ops:
  12.6 46.7 %gather.6 = bf16[4,4,4,4,16,1024]{5,4,3,2,1,0:T(8,128)(2,1)} custom-call(bf16[4,16,1024]{2,1,0:T(8,128)(2,1)} %get-tuple-element.9.src), custom_call_target="tpu_custom_call" | custom-call | tf_op jit(solution)/shard_map/gather/pallas_call | solution.py:146
  63.6 6.7 multiply_convert_fusion.5
  72.7 6.7 multiply_convert_fusion.4
  88.1 40.9 %gather.7 = bf16[4,4,4,4,16,1024]{5,4,3,2,1,0:T(8,128)(2,1)} custom-call(bf16[4,16,1024]{2,1,0:T(8,128)(2,1)} %get-tuple-element.8.src), custom_call_target="tpu_custom_call" | custom-call | tf_op jit(solution)/shard_map/gather/pallas_call | solution.py:146
  153.1 5.7 collective-permute-start.3
  158.8 42.1 %gather.8 = bf16[4,4,4,4,16,1024]{5,4,3,2,1,0:T(8,128)(2,1)} custom-call(bf16[4,16,1024]{2,1,0:T(8,128)(2,1)} %get-tuple-element.7.src), custom_call_target="tpu_custom_call" | custom-call | tf_op jit(solution)/shard_map/gather/pallas_call | solution.py:146
  227.7 6.5 collective-permute-done.4
  236.8 40.9 %gather.9 = bf16[4,4,4,4,16,1024]{5,4,3,2,1,0:T(8,128)(2,1)} custom-call(bf16[4,16,1024]{2,1,0:T(8,128)(2,1)} %get-tuple-element.7.src), custom_call_target="tpu_custom_call" | custom-call | tf_op jit(solution)/shard_map/gather/pallas_call | solution.py:146
  282.3 6.2 fusion.5
  291.5 6.2 fusion.11
  300.1 5.4 collective-permute-start.6
  305.5 6.1 fusion.44
  316.1 42.2 %gather.10 = bf16[4,4,4,4,16,1024]{5,4,3,2,1,0:T(8,128)(2,1)} custom-call(bf16[4,16,1024]{2,1,0:T(8,128)(2,1)} %get-tuple-element.8.src), custom_call_target="tpu_custom_call" | custom-call | tf_op jit(solution)/shard_map/gather/pallas_call | solution.py:146
  392.0 6.7 pad_maximum_fusion.4
  398.7 74.1 %scatter_sum.5 = f32[4,16,1024]{2,1,0:T(8,128)} custom-call(f32[2,4,4,4,16,1024]{5,4,3,2,1,0:T(8,128)} %get-tuple-element.55.up, f32[2,4,4,4,16,1024]{5,4,3,2,1,0:T(8,128)} %get-tuple-element.56.down), custom_call_target="tpu_custom_call" | custom-call | tf_op jit(solution)/shard_map/scatter_sum/pallas_call | solution.py:257
  472.8 6.2 fusion.66
  497.0 39.9 %gather.11 = bf16[4,4,4,4,16,1024]{5,4,3,2,1,0:T(8,128)(2,1)} custom-call(bf16[4,16,1024]{2,1,0:T(8,128)(2,1)} %get-tuple-element.9.src), custom_call_target="tpu_custom_call" | custom-call | tf_op jit(solution)/shard_map/gather/pallas_call | solution.py:146
  556.4 6.4 collective-permute-start.8
  562.9 7.1 pad_maximum_fusion.2
  569.9 68.3 %scatter_sum.4 = f32[4,16,1024]{2,1,0:T(8,128)} custom-call(f32[2,4,4,4,16,1024]{5,4,3,2,1,0:T(8,128)} %get-tuple-element.57.up, f32[2,4,4,4,16,1024]{5,4,3,2,1,0:T(8,128)} %get-tuple-element.58.down), custom_call_target="tpu_custom_call" | custom-call | tf_op jit(solution)/shard_map/scatter_sum/pallas_call | solution.py:257
  653.3 6.8 pad_maximum_fusion
  660.2 67.9 %scatter_sum.3 = f32[4,16,1024]{2,1,0:T(8,128)} custom-call(f32[2,4,4,4,16,1024]{5,4,3,2,1,0:T(8,128)} %get-tuple-element.59.up, f32[2,4,4,4,16,1024]{5,4,3,2,1,0:T(8,128)} %get-tuple-element.60.down), custom_call_target="tpu_custom_call" | custom-call | tf_op jit(solution)/shard_map/scatter_sum/pallas_call | solution.py:257
  734.8 10.1 %collective-permute-start.9 = (f32[3,2,8,64,16]{3,4,2,1,0:T(8,128)S(1)}, f32[3,2,8,64,16]{3,4,2,1,0:T(8,128)S(1)}, u32[]{:S(2)}, u32[]{:S(2)}) collective-permute-start(f32[3,2,8,64,16]{3,4,2,1,0:T(8,128)S(1)} %bitcast.176), channel_id=1, source_target_pairs={{0,1},{1,0},{2,3},{3,2},{4,5},{5,4},{6,7},{7,6},{8,9},{9,8},{10,11... | collective-permute-start | bytes 589832 | tf_op jit(solution)/shard_map/ppermute | solution.py:26
  752.8 5.5 reshape.119
  (164 shorter events, 199.7 us)
Async XLA Ops:
  0.6 63.0 %collective-permute-start = (bf16[512,1024]{1,0:T(8,128)(2,1)}, bf16[512,1024]{1,0:T(8,128)(2,1)}, u32[]{:S(2)}, u32[]{:S(2)}) collective-permute-start(bf16[512,1024]{1,0:T(8,128)(2,1)} %param.4), channel_id=1, source_target_pairs={{0,1},{1,0},{2,3},{3,2},{4,5},{5,4},{6,7},{7,6},{8,9},{9,8},{10,11... | collective-permute-start | bytes 3145736 | tf_op jit(solution)/shard_map/ppermute | solution.py:26
  10.0 1.7 collective-permute-start.1
  83.8 49.5 %collective-permute-start.2 = (f32[1024,1024]{1,0:T(8,128)}, f32[1024,1024]{1,0:T(8,128)}, u32[]{:S(2)}, u32[]{:S(2)}) collective-permute-start(f32[1024,1024]{1,0:T(8,128)} %convolution_add_fusion.5), channel_id=1, source_target_pairs={{0,1},{1,0},{2,3},{3,2},{4,5},{5,4},{6,7},{7,6},{8,9},{9,8},{10,11... | collective-permute-start | bytes 12582920 | tf_op jit(solution)/shard_map/ppermute | solution.py:26
  153.1 52.0 %collective-permute-start.3 = (f32[1024,1024]{1,0:T(8,128)}, f32[1024,1024]{1,0:T(8,128)}, u32[]{:S(2)}, u32[]{:S(2)}) collective-permute-start(f32[1024,1024]{1,0:T(8,128)} %convolution_add_fusion.4), channel_id=1, source_target_pairs={{0,1},{1,0},{2,3},{3,2},{4,5},{5,4},{6,7},{7,6},{8,9},{9,8},{10,11... | collective-permute-start | bytes 12582920 | tf_op jit(solution)/shard_map/ppermute | solution.py:26
  209.9 24.3 %copy-start.2 = (bf16[1024,1024]{1,0:T(8,128)(2,1)}, bf16[1024,1024]{1,0:T(8,128)(2,1)S(1)}, u32[]{:S(2)}) copy-start(bf16[1024,1024]{1,0:T(8,128)(2,1)S(1)} %add_convert_fusion.3) | copy-start | bytes 6291460
  220.6 6.8 copy-start.13
  223.0 11.2 %collective-permute-start.4 = (f32[1024,1024]{1,0:T(8,128)S(1)}, f32[1024,1024]{1,0:T(8,128)S(1)}, u32[]{:S(2)}, u32[]{:S(2)}) collective-permute-start(f32[1024,1024]{1,0:T(8,128)S(1)} %convolution_add_fusion.3), channel_id=1, source_target_pairs={{0,1},{1,0},{2,3},{3,2},{4,5},{5,4},{6,7},{7,6},{8,9},{9,8},{10,11... | collective-permute-start | bytes 12582920 | tf_op jit(solution)/shard_map/ppermute | solution.py:26
  227.4 54.3 %collective-permute-start.5 = (bf16[512,1024]{1,0:T(8,128)(2,1)S(1)}, bf16[512,1024]{1,0:T(8,128)(2,1)}, u32[]{:S(2)}, u32[]{:S(2)}) collective-permute-start(bf16[512,1024]{1,0:T(8,128)(2,1)S(1)} %copy-done.13), channel_id=1, source_target_pairs={{0,1},{1,0},{2,3},{3,2},{4,5},{5,4},{6,7},{7,6},{8,9},{9,8},{10,11... | collective-permute-start | bytes 3145736 | tf_op jit(solution)/shard_map/ppermute | solution.py:26
  297.7 7.8 %copy-start.21 = (bf16[1024,1024]{1,0:T(8,128)(2,1)S(1)}, bf16[1024,1024]{1,0:T(8,128)(2,1)}, u32[]{:S(2)}) copy-start(bf16[1024,1024]{1,0:T(8,128)(2,1)} %copy-done.20) | copy-start | bytes 6291460
  300.1 12.2 %collective-permute-start.6 = (f32[1024,1024]{1,0:T(8,128)S(1)}, f32[1024,1024]{1,0:T(8,128)S(1)}, u32[]{:S(2)}, u32[]{:S(2)}) collective-permute-start(f32[1024,1024]{1,0:T(8,128)S(1)} %convolution_add_fusion.2), channel_id=1, source_target_pairs={{0,1},{1,0},{2,3},{3,2},{4,5},{5,4},{6,7},{7,6},{8,9},{9,8},{10,11... | collective-permute-start | bytes 12582920 | tf_op jit(solution)/shard_map/ppermute | solution.py:26
  373.8 9.2 %copy-start.29 = (bf16[1024,1024]{1,0:T(8,128)(2,1)S(1)}, bf16[1024,1024]{1,0:T(8,128)(2,1)}, u32[]{:S(2)}) copy-start(bf16[1024,1024]{1,0:T(8,128)(2,1)} %copy-done.28) | copy-start | bytes 6291460
  378.2 8.8 %copy-start.3 = (bf16[1024,1024]{1,0:T(8,128)(2,1)S(1)}, bf16[1024,1024]{1,0:T(8,128)(2,1)}, u32[]{:S(2)}) copy-start(bf16[1024,1024]{1,0:T(8,128)(2,1)} %copy-done.2) | copy-start | bytes 6291460
  378.2 8.8 %copy-start.35 = (bf16[1024,1024]{1,0:T(8,128)(2,1)S(1)}, bf16[1024,1024]{1,0:T(8,128)(2,1)}, u32[]{:S(2)}) copy-start(bf16[1024,1024]{1,0:T(8,128)(2,1)} %copy-done.34) | copy-start | bytes 6291460
  378.2 114.0 %collective-permute-start.7 = (f32[1024,1024]{1,0:T(8,128)}, f32[1024,1024]{1,0:T(8,128)}, u32[]{:S(2)}, u32[]{:S(2)}) collective-permute-start(f32[1024,1024]{1,0:T(8,128)} %convolution_add_fusion.1), channel_id=1, source_target_pairs={{0,1},{1,0},{2,3},{3,2},{4,5},{5,4},{6,7},{7,6},{8,9},{9,8},{10,11... | collective-permute-start | bytes 12582920 | tf_op jit(solution)/shard_map/ppermute | solution.py:26
  497.0 145.4 %copy-start.5 = (bf16[1024,1024]{1,0:T(8,128)(2,1)}, bf16[1024,1024]{1,0:T(8,128)(2,1)S(1)}, u32[]{:S(2)}) copy-start(bf16[1024,1024]{1,0:T(8,128)(2,1)S(1)} %add_convert_fusion) | copy-start | bytes 6291460
  551.8 11.0 %copy-start.7 = (f32[1024,1024]{1,0:T(8,128)S(1)}, f32[1024,1024]{1,0:T(8,128)}, u32[]{:S(2)}) copy-start(f32[1024,1024]{1,0:T(8,128)} %fusion.66) | copy-start | bytes 12582916
  551.8 11.0 %copy-start.8 = (f32[1024,1024]{1,0:T(8,128)S(1)}, f32[1024,1024]{1,0:T(8,128)}, u32[]{:S(2)}) copy-start(f32[1024,1024]{1,0:T(8,128)} %fusion.65) | copy-start | bytes 12582916
  551.8 11.0 %copy-start.9 = (f32[1024,1024]{1,0:T(8,128)S(1)}, f32[1024,1024]{1,0:T(8,128)}, u32[]{:S(2)}) copy-start(f32[1024,1024]{1,0:T(8,128)} %fusion.68) | copy-start | bytes 12582916
  551.8 11.0 %copy-start.10 = (f32[1024,1024]{1,0:T(8,128)S(1)}, f32[1024,1024]{1,0:T(8,128)}, u32[]{:S(2)}) copy-start(f32[1024,1024]{1,0:T(8,128)} %fusion.67) | copy-start | bytes 12582916
  556.4 201.9 %collective-permute-start.8 = (f32[1024,1024]{1,0:T(8,128)}, f32[1024,1024]{1,0:T(8,128)}, u32[]{:S(2)}, u32[]{:S(2)}) collective-permute-start(f32[1024,1024]{1,0:T(8,128)} %convolution_add_fusion), channel_id=1, source_target_pairs={{0,1},{1,0},{2,3},{3,2},{4,5},{5,4},{6,7},{7,6},{8,9},{9,8},{10,11... | collective-permute-start | bytes 12582920 | tf_op jit(solution)/shard_map/ppermute | solution.py:26
  660.2 67.9 %copy-start.11 = (f32[4,16,1024]{2,1,0:T(8,128)S(1)}, f32[4,16,1024]{2,1,0:T(8,128)}, u32[]{:S(2)}) copy-start(f32[4,16,1024]{2,1,0:T(8,128)} %scatter_sum.5) | copy-start | bytes 786436
  660.2 67.9 %copy-start.12 = (f32[4,16,1024]{2,1,0:T(8,128)S(1)}, f32[4,16,1024]{2,1,0:T(8,128)}, u32[]{:S(2)}) copy-start(f32[4,16,1024]{2,1,0:T(8,128)} %scatter_sum.4) | copy-start | bytes 786436
  732.9 14.4 %copy-start.4 = (f32[3,2,1,8,64,16]{5,4,3,2,1,0:T(8,128)S(1)}, f32[3,2,1,8,64,16]{5,4,3,2,1,0:T(8,128)}, u32[]{:S(2)}) copy-start(f32[3,2,1,8,64,16]{5,4,3,2,1,0:T(8,128)} %get-tuple-element.34) | copy-start | bytes 589828
  734.8 12.8 %collective-permute-start.9 = (f32[3,2,8,64,16]{3,4,2,1,0:T(8,128)S(1)}, f32[3,2,8,64,16]{3,4,2,1,0:T(8,128)S(1)}, u32[]{:S(2)}, u32[]{:S(2)}) collective-permute-start(f32[3,2,8,64,16]{3,4,2,1,0:T(8,128)S(1)} %bitcast.176), channel_id=1, source_target_pairs={{0,1},{1,0},{2,3},{3,2},{4,5},{5,4},{6,7},{7,6},{8,9},{9,8},{10,11... | collective-permute-start | bytes 589832 | tf_op jit(solution)/shard_map/ppermute | solution.py:26
  (31 other events, 111.8 us)

commit v2 on v0

v2 whole, which is shorter than its diff:
```python
import functools
import math

import jax
import jax.numpy as jnp
from jax import lax
from jax.experimental import pallas as pl
from jax.experimental.pallas import tpu as pltpu
from jax.sharding import Mesh, PartitionSpec as P

CHIPS = ("z", "y", "x")
ALL = CHIPS + ("c",)
BF16 = jnp.bfloat16
F32 = jnp.float32
SIDE = 4
ROWS = 16
TILE = 256
WIDE = 512
INV_SQRT_2PI = (2.0 * math.pi) ** -0.5
VMEM_LIMIT = 63 * 1024 * 1024
MESH = pl.DeviceIdType.MESH
ORDERS = (("x", "y", "z"), ("y", "z", "x"), ("z", "x", "y"))


def gelu_parts(pre_act):
    norm_cdf = 0.5 * (1.0 + lax.erf(pre_act * (2.0 ** -0.5)))
    norm_pdf = jnp.exp(-0.5 * pre_act * pre_act) * INV_SQRT_2PI
    return pre_act * norm_cdf, norm_cdf + pre_act * norm_pdf


def swap(val):
    return lax.ppermute(val, "c", [(0, 1), (1, 0)])


def pair_rows(own, core):
    got = swap(own)
    return jnp.where(core == 0, jnp.concatenate([own, got], 0), jnp.concatenate([got, own], 0))


def jobs_of(width):
    tile = width // 8
    cuts = ((0, 3 * tile), (3 * tile, 3 * tile), (6 * tile, 2 * tile))
    return [(3, cuts[k], ORDERS[k]) for k in range(3)] + [(mat, (0, width), ORDERS[mat]) for mat in range(3)]


SMALL, LARGE = range(3), range(3, 6)


def view(ref, lead, axes, sel, cols=None):
    mid = tuple(sel.get(a, slice(None)) for a in axes)
    last = (slice(None), pl.ds(*cols)) if cols is not None else ()
    return ref.at[lead + mid + last]


def half(axis, k):
    return {axis: pl.ds(2 * k, 2)}


def ring_places():
    me = {a: lax.axis_index(a) for a in CHIPS}
    near = {a: [lax.rem(me[a] + d, SIDE) for d in range(SIDE)] for a in CHIPS}
    return me, near


def enter(near, ring=True, partner=None):
    barrier = pltpu.get_barrier_semaphore()
    if ring:
        for axis in CHIPS:
            for d in (1, 3):
                pl.semaphore_signal(barrier, inc=1, device_id={axis: near[axis][d]}, device_id_type=MESH)
    if partner is not None:
        pl.semaphore_signal(barrier, inc=1, device_id={"c": partner}, device_id_type=MESH)
    pl.semaphore_wait(barrier, 6 * ring + (partner is not None))


class Sender:
    def __init__(self, near, send_sem, recv_sem):
        self.near, self.send_sem, self.recv_sem, self.open = near, send_sem, recv_sem, {}

    def put(self, key, src, dst, axis, step):
        copy = pltpu.make_async_remote_copy(
            src_ref=src, dst_ref=dst, send_sem=self.send_sem.at[key], recv_sem=self.recv_sem.at[key],
            device_id={axis: self.near[axis][step]}, device_id_type=MESH)
        copy.start()
        self.open[key] = copy

    def got(self, key):
        self.open[key].wait_recv()

    def close(self):
        for copy in self.open.values():
            copy.wait_send()


RING_SEMS = [pltpu.SemaphoreType.DMA((6, 3, 6)), pltpu.SemaphoreType.DMA((6, 3, 6))]


class Gather:
    def __init__(self, width, me, near, buf, send_sem, recv_sem):
        self.me, self.near, self.buf, self.jobs = me, near, buf, jobs_of(width)
        self.net = Sender(near, send_sem, recv_sem)

    def push(self, job, phase, slot, d, part, step):
        mat, cols, order = self.jobs[job]
        axis = order[2 - phase]
        sel = {a: self.me[a] for a in order[:2 - phase]}
        sel[axis] = self.near[axis][d]
        if part is not None:
            sel.update(half(order[3 - phase], part))
        here = view(self.buf, (mat,), CHIPS, sel, cols)
        self.net.put((job, phase, slot), here, here, axis, step)

    def send(self, phase):
        for job in range(6):
            if phase == 0:
                self.push(job, phase, 0, 0, None, 1)
                self.push(job, phase, 1, 0, None, 3)
            else:
                self.push(job, phase, 0, 0, 0, 1)
                self.push(job, phase, 1, 0, 1, 3)
                self.push(job, phase, 2, 0, 1, 1)
                self.push(job, phase, 3, 0, 0, 3)

    def forward(self, phase):
        for job in range(6):
            self.net.got((job, phase, 0))
            if phase == 0:
                self.push(job, phase, 2, 3, None, 1)
            else:
                self.push(job, phase, 4, 3, 0, 1)
                self.net.got((job, phase, 1))
                self.push(job, phase, 5, 1, 1, 3)

    def finish(self, phase):
        for job in range(6):
            for slot in ((1, 2) if phase == 0 else (2, 3, 4, 5)):
                self.net.got((job, phase, slot))

    def begin(self):
        for phase in range(2):
            self.send(phase)
            self.forward(phase)
            self.finish(phase)
        self.send(2)


def gather_kernel(width, src, out, buf, send_sem, recv_sem, loc_sem, out_sem):
    me, near = ring_places()
    first = pltpu.make_async_copy(src, view(buf, (slice(None),), CHIPS, me), loc_sem.at[0])
    first.start()
    enter(near)
    first.wait()
    ring = Gather(width, me, near, buf, send_sem, recv_sem)
    ring.begin()
    ring.forward(2)
    ring.finish(2)
    last = pltpu.make_async_copy(buf, out, out_sem.at[0])
    last.start()
    last.wait()
    ring.net.close()


def gather(packed, call_id):
    width = packed.shape[-1]
    full = (4, SIDE, SIDE, SIDE, ROWS, width)
    return pl.pallas_call(
        functools.partial(gather_kernel, width),
        out_shape=jax.ShapeDtypeStruct(full, packed.dtype),
        in_specs=[pl.BlockSpec(memory_space=pl.ANY)],
        out_specs=pl.BlockSpec(memory_space=pl.ANY),
        scratch_shapes=[pltpu.VMEM(full, packed.dtype)] + RING_SEMS
        + [pltpu.SemaphoreType.DMA((1,)), pltpu.SemaphoreType.DMA((1,))],
        compiler_params=pltpu.CompilerParams(collective_id=call_id, has_side_effects=True),
        name="gather",
    )(packed)


def dot_nn(left, right):
    return lax.dot_general(left, right, (((1,), (0,)), ((), ())), preferred_element_type=F32)


def dot_nt(left, right):
    return lax.dot_general(left, right, (((1,), (1,)), ((), ())), preferred_element_type=F32)


def dot_tn(left, right):
    return lax.dot_general(left, right, (((0,), (0,)), ((), ())), preferred_element_type=F32)


def layer_kernel(forward, width, with_gather, *refs):
    refs = list(refs)
    stream, weights = refs.pop(0), refs.pop(0)
    slope_in = None if forward else refs.pop(0)
    packed = refs.pop(0) if with_gather else None
    result = refs.pop(0)
    act_out = refs.pop(0)
    slope_out = refs.pop(0) if forward else None
    next_out = refs.pop(0) if with_gather else None
    cur, mats, act, slope, part, got, pair_send, pair_recv, loc_sem, out_sem = refs[:10]
    tokens = cur.shape[0]
    tiles = tokens // TILE
    me, near = ring_places()
    partner = 1 - lax.axis_index("c")
    loads = [pltpu.make_async_copy(stream, cur, loc_sem.at[0]), pltpu.make_async_copy(weights, mats, loc_sem.at[1])]
    if not forward:
        loads.append(pltpu.make_async_copy(slope_in, slope, loc_sem.at[2]))
    if with_gather:
        buf, send_sem, recv_sem = refs[10:]
        ring = Gather(width, me, near, buf, send_sem, recv_sem)
        own = pltpu.make_async_copy(packed, view(buf, (slice(None),), CHIPS, me), loc_sem.at[3])
        own.start()
    for copy in loads:
        copy.start()
    enter(near, with_gather, partner)
    if with_gather:
        own.wait()
        ring.begin()
    for copy in loads:
        copy.wait()

    def exchange(tile):
        rows = pl.ds(tile * TILE, TILE)
        return pltpu.make_async_remote_copy(
            src_ref=part.at[rows], dst_ref=got.at[rows], send_sem=pair_send.at[tile], recv_sem=pair_recv.at[tile],
            device_id={"c": partner}, device_id_type=MESH)

    def compute(tile, _):
        rows = pl.ds(pl.multiple_of(tile * TILE, TILE), TILE)
        left = cur[rows, :]
        for block in range(2):
            for cut in range(width // WIDE):
                cols = pl.ds(block * width + cut * WIDE, WIDE)
                if forward:
                    pre = dot_nn(left, mats[block * width:(block + 1) * width, cut * WIDE:(cut + 1) * WIDE])
                    act_val, slope_val = gelu_parts(pre)
                    act[rows, cols] = act_val.astype(BF16)
                    slope[rows, cols] = slope_val
                else:
                    low = (2 + block) * width + cut * WIDE
                    d_act = dot_nt(left, mats[low:low + WIDE, :])
                    act[rows, cols] = (d_act * slope[rows, cols]).astype(BF16)
        if forward:
            part[rows, :] = dot_nn(act[rows, :], mats[2 * width:, :])
        else:
            part[rows, :] = dot_nt(act[rows, :width], mats[:width, :]) + dot_nt(act[rows, width:], mats[width:2 * width, :])
        exchange(tile).start()
        return 0

    saves = []

    def save(k, low, high):
        rows = pl.ds(low * TILE, (high - low) * TILE)
        pairs = [(act, act_out)] + ([(slope, slope_out)] if forward else [])
        for n, (src, dst) in enumerate(pairs):
            saves.append(pltpu.make_async_copy(src.at[rows], dst.at[rows], out_sem.at[2 * k + n]))
            saves[-1].start()

    mid = tiles // 2
    lax.fori_loop(0, mid, compute, 0)
    save(0, 0, mid)
    if with_gather:
        ring.forward(2)
    lax.fori_loop(mid, tiles, compute, 0)
    save(1, mid, tiles)
    for tile in range(tiles):
        exchange(tile).wait_recv()
        rows = pl.ds(tile * TILE, TILE)
        result[rows, :] = (cur[rows, :].astype(F32) + (part[rows, :] + got[rows, :])).astype(BF16)
    if with_gather:
        ring.finish(2)
        last = pltpu.make_async_copy(buf, next_out, out_sem.at[4])
        last.start()
        last.wait()
        ring.net.close()
    for copy in saves:
        copy.wait()
    for tile in range(tiles):
        exchange(tile).wait_send()


def layer_call(forward, stream, full, slope, packed, call_id):
    tokens, width = stream.shape
    hidden = 2 * width
    with_gather = packed is not None
    shape = jax.ShapeDtypeStruct
    whole = (4, SIDE, SIDE, SIDE, ROWS, width)
    args = [stream, full.reshape(4 * width, width)] + ([] if forward else [slope]) + ([packed] if with_gather else [])
    outs = [shape((tokens, width), BF16), shape((tokens, hidden), BF16)]
    outs += ([shape((tokens, hidden), F32)] if forward else []) + ([shape(whole, BF16)] if with_gather else [])
    tiles = tokens // TILE
    return pl.pallas_call(
        functools.partial(layer_kernel, forward, width, with_gather),
        out_shape=outs,
        in_specs=[pl.BlockSpec(memory_space=pl.ANY)] * len(args),
        out_specs=[pl.BlockSpec(memory_space=pltpu.VMEM)] + [pl.BlockSpec(memory_space=pl.ANY)] * (len(outs) - 1),
        scratch_shapes=[pltpu.VMEM((tokens, width), BF16), pltpu.VMEM((4 * width, width), BF16),
                        pltpu.VMEM((tokens, hidden), BF16), pltpu.VMEM((tokens, hidden), F32),
                        pltpu.VMEM((tokens, width), F32), pltpu.VMEM((tokens, width), F32),
                        pltpu.SemaphoreType.DMA((tiles,)), pltpu.SemaphoreType.DMA((tiles,)),
                        pltpu.SemaphoreType.DMA((4,)), pltpu.SemaphoreType.DMA((5,))]
        + ([pltpu.VMEM(whole, BF16)] + RING_SEMS if with_gather else []),
        compiler_params=pltpu.CompilerParams(collective_id=call_id, has_side_effects=True, vmem_limit_bytes=VMEM_LIMIT),
        cost_estimate=pl.CostEstimate(flops=8 * tokens * hidden * width, bytes_accessed=40 << 20, transcendentals=0),
        name="forward_layer" if forward else "backward_layer",
    )(*args)


def add_into(dst, src, lead):
    if not lead:
        dst[...] = dst[...] + src[...]
        return

    def step(k, _):
        add_into(dst.at[k], src.at[k], lead[1:])
        return 0

    lax.fori_loop(0, lead[0], step, 0)


class RingSum:
    def __init__(self, width, me, near, buf, recv, send_sem, recv_sem):
        self.me, self.near, self.buf, self.recv, self.jobs = me, near, buf, recv, jobs_of(width)
        self.net = Sender(near, send_sem, recv_sem)

    def here(self, job, phase, d, part=None):
        mat, cols, order = self.jobs[job]
        sel = {a: self.me[a] for a in order[:phase]}
        sel[order[phase]] = self.near[order[phase]][d]
        if part is not None:
            sel.update(half(order[phase + 1], part))
        return view(self.buf, (mat,), CHIPS, sel, cols)

    def there(self, job, phase, slot, part=None):
        order = self.jobs[job][2]
        left = [a for a in CHIPS if a not in order[:phase + 1]]
        return view(self.recv[3 * job + phase], (slot,), left, {} if part is None else half(order[phase + 1], part))

    def lead(self, job, phase, part=None):
        order = self.jobs[job][2]
        return [2 if part is not None and a == order[phase + 1] else SIDE for a in CHIPS if a not in order[:phase + 1]]

    def push(self, job, phase, slot, d, part, to_slot, step):
        self.net.put((job, phase, slot), self.here(job, phase, d, part), self.there(job, phase, to_slot, part),
                     self.jobs[job][2][phase], step)

    def send(self, job, phase):
        if phase == 2:
            self.push(job, phase, 0, 2, None, 0, 1)
            self.push(job, phase, 3, 3, None, 2, 3)
        else:
            self.push(job, phase, 0, 2, 0, 0, 1)
            self.push(job, phase, 1, 2, 1, 0, 3)
            self.push(job, phase, 2, 1, 1, 1, 1)
            self.push(job, phase, 3, 3, 0, 2, 3)

    def mid(self, job, phase):
        self.net.got((job, phase, 0))
        if phase == 2:
            add_into(self.here(job, phase, 1), self.there(job, phase, 0), [])
            self.push(job, phase, 2, 1, None, 1, 1)
        else:
            add_into(self.here(job, phase, 1, 0), self.there(job, phase, 0, 0), self.lead(job, phase, 0))
            self.push(job, phase, 4, 1, 0, 1, 1)
            self.net.got((job, phase, 1))
            add_into(self.here(job, phase, 3, 1), self.there(job, phase, 0, 1), self.lead(job, phase, 1))
            self.push(job, phase, 5, 3, 1, 2, 3)

    def finish(self, job, phase):
        for slot in ((2, 3) if phase == 2 else (2, 3, 4, 5)):
            self.net.got((job, phase, slot))
        add_into(self.here(job, phase, 0), self.there(job, phase, 1), self.lead(job, phase))
        add_into(self.here(job, phase, 0), self.there(job, phase, 2), self.lead(job, phase))


def recv_blocks(width):
    blocks = []
    for mat, cols, order in jobs_of(width):
        blocks += [pltpu.VMEM((3,) + (SIDE,) * (2 - phase) + (ROWS, cols[1]), F32) for phase in range(3)]
    return blocks


def sum_kernel(width, x_ref, act_ref, d_pre_ref, g_ref, out, x_val, act_val, d_pre, g_val, buf, *rest):
    send_sem, recv_sem, loc_sem = rest[18:]
    me, near = ring_places()
    ring = RingSum(width, me, near, buf, rest[:18], send_sem, recv_sem)
    loads = [pltpu.make_async_copy(src, dst, loc_sem.at[k]) for k, (src, dst) in enumerate(
        ((act_ref, act_val), (g_ref, g_val), (x_ref, x_val), (d_pre_ref, d_pre)))]
    for copy in loads:
        copy.start()
    enter(near)

    def grad(mat):
        def slab(z, _):
            if mat < 2:
                cols = pl.ds(pl.multiple_of(z * (width // SIDE), width // SIDE), width // SIDE)
                val = dot_tn(x_val[:, cols], d_pre[:, mat * width:(mat + 1) * width])
            else:
                cols = pl.ds(pl.multiple_of((mat - 2) * width + z * (width // SIDE), width // SIDE), width // SIDE)
                val = dot_tn(act_val[:, cols], g_val[...])
            buf[mat, z] = val.reshape(SIDE, SIDE, ROWS, width)
            return 0

        lax.fori_loop(0, SIDE, slab, 0)

    loads[0].wait()
    loads[1].wait()
    grad(3)
    for job in SMALL:
        ring.send(job, 0)
    grad(2)
    ring.send(5, 0)
    loads[2].wait()
    loads[3].wait()
    for mat in range(2):
        grad(mat)
        ring.send(3 + mat, 0)
    for job in SMALL:
        ring.mid(job, 0)
    for job in LARGE:
        ring.mid(job, 0)
    for phase in range(3):
        for group in (SMALL, LARGE):
            for job in group:
                ring.finish(job, phase)
                if phase < 2:
                    ring.send(job, phase + 1)
        if phase < 2:
            for group in (SMALL, LARGE):
                for job in group:
                    ring.mid(job, phase + 1)
    for mat in range(4):
        out[mat] = view(buf, (mat,), CHIPS, me)[...]
    ring.net.close()


def scatter_sum(x_in, act, d_pre, g_in, call_id):
    tokens, width = x_in.shape
    return pl.pallas_call(
        functools.partial(sum_kernel, width),
        out_shape=jax.ShapeDtypeStruct((4, ROWS, width), F32),
        in_specs=[pl.BlockSpec(memory_space=pl.ANY)] * 4,
        out_specs=pl.BlockSpec(memory_space=pltpu.VMEM),
        scratch_shapes=[pltpu.VMEM((tokens, width), BF16), pltpu.VMEM((tokens, 2 * width), BF16),
                        pltpu.VMEM((tokens, 2 * width), BF16), pltpu.VMEM((tokens, width), BF16),
                        pltpu.VMEM((4, SIDE, SIDE, SIDE, ROWS, width), F32)] + recv_blocks(width)
        + RING_SEMS + [pltpu.SemaphoreType.DMA((4,))],
        compiler_params=pltpu.CompilerParams(collective_id=call_id, has_side_effects=True, vmem_limit_bytes=VMEM_LIMIT),
        cost_estimate=pl.CostEstimate(flops=8 * tokens * width * width, bytes_accessed=12 << 20, transcendentals=0),
        name="scatter_sum",
    )(x_in, act, d_pre, g_in)


def pack_weights(up_loc, down_loc, core):
    layers, up_rows, hidden = up_loc.shape
    by_core = up_loc.reshape(layers, up_rows, 64, 2, 2, 16)
    mine = lax.dynamic_index_in_dim(by_core, core, 3, keepdims=False)
    other = lax.dynamic_index_in_dim(by_core, 1 - core, 3, keepdims=False)
    mine, other = (v.transpose(0, 3, 1, 2, 4).reshape(layers, 2, up_rows, hidden // 4) for v in (mine, other))
    got = swap(other)
    up = jnp.where(core == 0, jnp.concatenate([mine, got], 2), jnp.concatenate([got, mine], 2))
    return jnp.concatenate([up, down_loc.reshape(layers, 2, 16, -1)], 1)


def unpack_up_grad(grad, core):
    layers = grad.shape[0]
    rows = grad.reshape(layers, 2, 2, 8, 64, 16)
    mine = lax.dynamic_index_in_dim(rows, core, 2, keepdims=False)
    got = swap(lax.dynamic_index_in_dim(rows, 1 - core, 2, keepdims=False))
    both = jnp.where(core == 0, jnp.stack([mine, got]), jnp.stack([got, mine]))
    return both.transpose(1, 3, 4, 0, 2, 5).reshape(layers, 8, 4096)


def solution(mesh):
    grid = Mesh(mesh.devices.reshape(SIDE, SIDE, SIDE, 2), ALL)
    tok_spec = P(ALL, None)
    weight_spec = P(None, ALL, None)

    def device_step(x_loc, up_loc, down_loc, g_loc):
        layers = up_loc.shape[0]
        tokens = x_loc.shape[0]
        core = lax.axis_index("c")
        packed = pack_weights(up_loc, down_loc, core)
        x_cur = pair_rows(x_loc, core)
        g_cur = pair_rows(g_loc, core)
        saved = []
        full = gather(packed[0], 0)
        for layer in range(layers):
            following = packed[layer + 1] if layer + 1 < layers else lax.optimization_barrier((packed[layer], x_cur))[0]
            x_in = x_cur
            x_cur, act, slope, full = layer_call(True, x_in, full, None, following, 1 + layer)
            saved.append((x_in, act, slope))
        y_out = lax.dynamic_slice_in_dim(x_cur, core * tokens, tokens, 0)
        grads = [None] * layers
        for layer in reversed(range(layers)):
            x_in, act, slope = saved[layer]
            g_in = g_cur
            if layer:
                following = lax.optimization_barrier((packed[layer - 1], x_cur))[0]
                g_cur, d_pre, full = layer_call(False, g_in, full, slope, following, 4 + layer)
            else:
                g_cur, d_pre = layer_call(False, g_in, full, slope, None, 4 + layer)
            grads[layer] = scatter_sum(x_in, act, d_pre, g_in, 7 + layer)
        grads = jnp.stack(grads)
        grad_up = unpack_up_grad(grads[:, :2], core)
        grad_in = lax.dynamic_slice_in_dim(g_cur, core * tokens, tokens, 0)
        return y_out, grad_in, grad_up, grads[:, 2:].reshape(layers, 32, -1)

    return jax.shard_map(device_step, mesh=grid, in_specs=(tok_spec, weight_spec, weight_spec, tok_spec),
                         out_specs=(tok_spec, tok_spec, weight_spec, weight_spec), check_vma=False)
```

time: 4630 us -> 588 us (0.13)
  waiting for transfers between devices: 4380 us -> 0.01 us
  Pallas kernels: 0 us -> 538 us
  matrix products: 181 us -> 0 us
    reduce_scatter x3 -> x0, waiting for transfers between devices: 2000 us -> none  [device_step(): lax.psum_scatter(grad_down, all_axes, scatter_dimension=0, tiled=True)]
    unnamed x17 -> x0, waiting for transfers between devices: 1860 us -> none
    pallas_call x0 -> x10, Pallas kernels: none -> 538 us  [the longest x6 264 us: layer_call(): pl.pallas_call(functools.partial(layer_kernel, forward, width, with_gathe...]
    all_gather x8 -> x0, waiting for transfers between devices: 514 us -> none  [the longest x3 201 us: device_step(): full_up = lax.all_gather(up_loc[layer], all_axes, axis=0, tiled=True)]
    dot_general x16 -> x0, matrix products: 164 us -> none  [contract(): lax.dot_general(left, right, (((left_dim,), (right_dim,)), ((), ())), pre...]
  transfers between devices with their start and end apart: 14 -> 4, of which waited for: 14 -> 0; matrix products, arithmetic and copies ran while one was open for 4% -> 3% of each run, Pallas kernels for 0% -> 8%
where the time goes in v2:
time: 588 us; the launch traced here: 582 us
  Pallas kernels  538 us (91%)
  local copies, waits for them, and re-layouts  29.7 us (5%)
  other arithmetic  7.78 us (1%)
    pallas_call x6, Pallas kernels, layer_call(): pl.pallas_call(functools.partial(layer_kernel, forward, width, with_gathe...  264 us
    pallas_call x3, Pallas kernels, scatter_sum(): pl.pallas_call(functools.partial(sum_kernel, width), out_shape=jax.ShapeD...  228 us
    pallas_call x1, Pallas kernels, gather(): pl.pallas_call(functools.partial(gather_kernel, width), out_shape=jax.Sha...  46.3 us
  transfers between devices with their start and end apart: 4, of which 0 were waited for; matrix products, arithmetic and copies ran while one was open for 3% of the time, Pallas kernels for 8%

profile of v2, /device:TPU:1, one launch (start us, length us, event | category | flops | bytes accessed | tf_op | source)
XLA Modules:
  0.0 581.7 jit_solution(14550701069075823838)
XLA Ops:
  0.6 1.4 collective-permute-start
  2.2 5.4 reshape.48
  7.6 1.1 constant_dynamic-slice_fusion.5
  8.9 1.2 reshape.50
  10.8 1.2 reshape.49
  12.9 46.3 %gather.1 = bf16[4,4,4,4,16,1024]{5,4,3,2,1,0:T(8,128)(2,1)} custom-call(bf16[4,16,1024]{2,1,0:T(8,128)(2,1)} %get-tuple-element.39.src.refs_3_), custom_call_target="tpu_custom_call" | custom-call | tf_op jit(solution)/shard_map/gather/pallas_call | solution.py:166
  59.2 5.0 maximum_select_fusion
  64.2 50.8 %forward_layer.3 = (bf16[1024,1024]{1,0:T(8,128)(2,1)}, bf16[1024,2048]{1,0:T(8,128)(2,1)}, f32[1024,2048]{1,0:T(8,128)}, bf16[4,4,4,4,16,1024]{5,4,3,2,1,0:T(8,128)(2,1)}) custom-call(bf16[1024,1024]{1,0:T(8,128)(2,1)} %get-tuple-element.59.refs_0_.x_ref, bf16[4096,1024]{1,0:T(8,128)(2,1)} %bitcast.38, bf16[4,16,1024]{2,1,0:T(8,128)(2,1)} %get-tuple-element.35.refs_2_.refs_3_), custom_call_target="tpu_custom_call" | custom-call | flops 17179869184 | bytes 41943040 | tf_op jit(solution)/shard_map/forward_layer/pallas_call | solution.py:291
  115.0 47.8 %forward_layer.4 = (bf16[1024,1024]{1,0:T(8,128)(2,1)}, bf16[1024,2048]{1,0:T(8,128)(2,1)}, f32[1024,2048]{1,0:T(8,128)}, bf16[4,4,4,4,16,1024]{5,4,3,2,1,0:T(8,128)(2,1)}) custom-call(bf16[1024,1024]{1,0:T(8,128)(2,1)} %get-tuple-element.27.refs_0_.x_ref, bf16[4096,1024]{1,0:T(8,128)(2,1)} %bitcast.52, bf16[4,16,1024]{2,1,0:T(8,128)(2,1)} %get-tuple-element.31.refs_2_), custom_call_target="tpu_custom_call" | custom-call | flops 17179869184 | bytes 41943040 | tf_op jit(solution)/shard_map/forward_layer/pallas_call | solution.py:291
  162.9 46.7 %forward_layer.5 = (bf16[1024,1024]{1,0:T(8,128)(2,1)}, bf16[1024,2048]{1,0:T(8,128)(2,1)}, f32[1024,2048]{1,0:T(8,128)}, bf16[4,4,4,4,16,1024]{5,4,3,2,1,0:T(8,128)(2,1)}) custom-call(bf16[1024,1024]{1,0:T(8,128)(2,1)} %get-tuple-element.29.refs_0_.x_ref, bf16[4096,1024]{1,0:T(8,128)(2,1)} %bitcast.53, bf16[4,16,1024]{2,1,0:T(8,128)(2,1)} %get-tuple-element.31.refs_2_), custom_call_target="tpu_custom_call" | custom-call | flops 17179869184 | bytes 41943040 | tf_op jit(solution)/shard_map/forward_layer/pallas_call | solution.py:291
  209.6 47.8 %backward_layer.3 = (bf16[1024,1024]{1,0:T(8,128)(2,1)}, bf16[1024,2048]{1,0:T(8,128)(2,1)}, bf16[4,4,4,4,16,1024]{5,4,3,2,1,0:T(8,128)(2,1)}) custom-call(bf16[1024,1024]{1,0:T(8,128)(2,1)} %get-tuple-element.60.refs_0_.g_ref, bf16[4096,1024]{1,0:T(8,128)(2,1)} %bitcast.51, f32[1024,2048]{1,0:T(8,128)} %get-tuple-element.34.refs_2_, ...), custom_call_target="tpu_custom_call" | custom-call | flops 17179869184 | bytes 41943040 | tf_op jit(solution)/shard_map/backward_layer/pallas_call | solution.py:291
  257.4 75.0 %scatter_sum.5 = f32[4,16,1024]{2,1,0:T(8,128)} custom-call(bf16[1024,1024]{1,0:T(8,128)(2,1)} %get-tuple-element.29.refs_0_.x_ref, bf16[1024,2048]{1,0:T(8,128)(2,1)} %get-tuple-element.48.act_ref, bf16[1024,2048]{1,0:T(8,128)(2,1)} %get-tuple-element.49.d_pre_ref, bf16[1024,1024]{1,0:T(8,128)(2,1)} %get-tuple-element.60.refs_0_.g_ref), custom_call_target="tpu_custom_call" | custom-call | flops 8589934592 | bytes 12582912 | tf_op jit(solution)/shard_map/scatter_sum/pallas_call | solution.py:438
  332.4 47.6 %backward_layer.4 = (bf16[1024,1024]{1,0:T(8,128)(2,1)}, bf16[1024,2048]{1,0:T(8,128)(2,1)}, bf16[4,4,4,4,16,1024]{5,4,3,2,1,0:T(8,128)(2,1)}) custom-call(bf16[1024,1024]{1,0:T(8,128)(2,1)} %get-tuple-element.36.refs_0_.g_ref, bf16[4096,1024]{1,0:T(8,128)(2,1)} %bitcast.49, f32[1024,2048]{1,0:T(8,128)} %get-tuple-element.38.refs_2_, ...), custom_call_target="tpu_custom_call" | custom-call | flops 17179869184 | bytes 41943040 | tf_op jit(solution)/shard_map/backward_layer/pallas_call | solution.py:291
  380.1 76.9 %scatter_sum.4 = f32[4,16,1024]{2,1,0:T(8,128)} custom-call(bf16[1024,1024]{1,0:T(8,128)(2,1)} %get-tuple-element.27.refs_0_.x_ref, bf16[1024,2048]{1,0:T(8,128)(2,1)} %get-tuple-element.46.act_ref, bf16[1024,2048]{1,0:T(8,128)(2,1)} %get-tuple-element.47.d_pre_ref, bf16[1024,1024]{1,0:T(8,128)(2,1)} %get-tuple-element.36.refs_0_.g_ref), custom_call_target="tpu_custom_call" | custom-call | flops 8589934592 | bytes 12582912 | tf_op jit(solution)/shard_map/scatter_sum/pallas_call | solution.py:438
  456.9 23.1 %backward_layer.5 = (bf16[1024,1024]{1,0:T(8,128)(2,1)}, bf16[1024,2048]{1,0:T(8,128)(2,1)}) custom-call(bf16[1024,1024]{1,0:T(8,128)(2,1)} %get-tuple-element.40.refs_0_.g_ref, bf16[4096,1024]{1,0:T(8,128)(2,1)} %bitcast.50, f32[1024,2048]{1,0:T(8,128)} %get-tuple-element.42.refs_2_), custom_call_target="tpu_custom_call" | custom-call | flops 17179869184 | bytes 41943040 | tf_op jit(solution)/shard_map/backward_layer/pallas_call | solution.py:291
  480.0 76.2 %scatter_sum.3 = f32[4,16,1024]{2,1,0:T(8,128)} custom-call(bf16[1024,1024]{1,0:T(8,128)(2,1)} %get-tuple-element.59.refs_0_.x_ref, bf16[1024,2048]{1,0:T(8,128)(2,1)} %get-tuple-element.44.act_ref, bf16[1024,2048]{1,0:T(8,128)(2,1)} %get-tuple-element.45.d_pre_ref, bf16[1024,1024]{1,0:T(8,128)(2,1)} %get-tuple-element.40.refs_0_.g_ref), custom_call_target="tpu_custom_call" | custom-call | flops 8589934592 | bytes 12582912 | tf_op jit(solution)/shard_map/scatter_sum/pallas_call | solution.py:438
  558.0 1.1 reshape.58
  559.1 1.9 constant_dynamic-slice_fusion.1
  561.0 2.0 copy.18
  563.0 2.6 collective-permute-start.3
  565.6 2.3 constant_dynamic-slice_fusion.3
  568.3 2.3 constant_dynamic-slice_fusion.2
  571.6 4.1 copy.19
  575.7 5.5 reshape.59
  (26 shorter events, 5.0 us)
Async XLA Ops:
  0.6 58.6 %collective-permute-start = (bf16[512,1024]{1,0:T(8,128)(2,1)}, bf16[512,1024]{1,0:T(8,128)(2,1)S(1)}, u32[]{:S(2)}, u32[]{:S(2)}) collective-permute-start(bf16[512,1024]{1,0:T(8,128)(2,1)} %param.4), channel_id=1, source_target_pairs={{0,1},{1,0},{2,3},{3,2},{4,5},{5,4},{6,7},{7,6},{8,9},{9,8},{10,11... | collective-permute-start | bytes 3145736 | tf_op jit(solution)/shard_map/ppermute | solution.py:32
  2.1 57.1 %collective-permute-start.2 = (bf16[512,1024]{1,0:T(8,128)(2,1)}, bf16[512,1024]{1,0:T(8,128)(2,1)}, u32[]{:S(2)}, u32[]{:S(2)}) collective-permute-start(bf16[512,1024]{1,0:T(8,128)(2,1)} %param.7), channel_id=1, source_target_pairs={{0,1},{1,0},{2,3},{3,2},{4,5},{5,4},{6,7},{7,6},{8,9},{9,8},{10,11... | collective-permute-start | bytes 3145736 | tf_op jit(solution)/shard_map/ppermute | solution.py:32
  8.7 3.4 copy-start.5
  10.1 1.9 collective-permute-start.1
  12.9 46.3 %copy-start.1 = (bf16[512,1024]{1,0:T(8,128)(2,1)S(1)}, bf16[512,1024]{1,0:T(8,128)(2,1)}, u32[]{:S(2)}) copy-start(bf16[512,1024]{1,0:T(8,128)(2,1)} %param.4) | copy-start | bytes 3145732
  12.9 46.3 %copy-start.2 = (bf16[512,1024]{1,0:T(8,128)(2,1)S(1)}, bf16[512,1024]{1,0:T(8,128)(2,1)}, u32[]{:S(2)}) copy-start(bf16[512,1024]{1,0:T(8,128)(2,1)} %param.7) | copy-start | bytes 3145732
  480.0 76.2 %copy-start.3 = (f32[4,16,1024]{2,1,0:T(8,128)S(1)}, f32[4,16,1024]{2,1,0:T(8,128)}, u32[]{:S(2)}) copy-start(f32[4,16,1024]{2,1,0:T(8,128)} %scatter_sum.5) | copy-start | bytes 786436
  480.0 76.2 %copy-start.4 = (f32[4,16,1024]{2,1,0:T(8,128)S(1)}, f32[4,16,1024]{2,1,0:T(8,128)}, u32[]{:S(2)}) copy-start(f32[4,16,1024]{2,1,0:T(8,128)} %scatter_sum.4) | copy-start | bytes 786436
  561.0 6.9 %copy-start = (f32[3,2,1,8,64,16]{5,4,3,2,1,0:T(8,128)S(1)}, f32[3,2,1,8,64,16]{5,4,3,2,1,0:T(8,128)}, u32[]{:S(2)}) copy-start(f32[3,2,1,8,64,16]{5,4,3,2,1,0:T(8,128)} %get-tuple-element.50) | copy-start | bytes 589828
  563.0 7.6 %collective-permute-start.3 = (f32[3,2,8,64,16]{3,4,2,1,0:T(8,128)S(1)}, f32[3,2,8,64,16]{3,4,2,1,0:T(8,128)S(1)}, u32[]{:S(2)}, u32[]{:S(2)}) collective-permute-start(f32[3,2,8,64,16]{3,4,2,1,0:T(8,128)S(1)} %bitcast.44), channel_id=1, source_target_pairs={{0,1},{1,0},{2,3},{3,2},{4,5},{5,4},{6,7},{7,6},{8,9},{9,8},{10,11... | collective-permute-start | bytes 589832 | tf_op jit(solution)/shard_map/ppermute | solution.py:32

commit v3 on v2

v3 whole, which is shorter than its diff:
```python
import functools
import math

import jax
import jax.numpy as jnp
from jax import lax
from jax.experimental import pallas as pl
from jax.experimental.pallas import tpu as pltpu
from jax.sharding import Mesh, PartitionSpec as P

CHIPS = ("z", "y", "x")
ALL = CHIPS + ("c",)
BF16 = jnp.bfloat16
F32 = jnp.float32
SIDE = 4
ROWS = 16
TILE = 256
WIDE = 512
INV_SQRT_2PI = (2.0 * math.pi) ** -0.5
VMEM_LIMIT = 63 * 1024 * 1024
MESH = pl.DeviceIdType.MESH
HERE, NEXT, OPPOSITE, PREV = range(4)
FULL = None
ORDERS = (("x", "y", "z"), ("y", "z", "x"), ("z", "x", "y"))


def gelu_parts(pre_act):
    norm_cdf = 0.5 * (1.0 + lax.erf(pre_act * (2.0 ** -0.5)))
    norm_pdf = jnp.exp(-0.5 * pre_act * pre_act) * INV_SQRT_2PI
    return pre_act * norm_cdf, norm_cdf + pre_act * norm_pdf


def jobs_of(width):
    tile = width // 8
    cuts = ((0, 3 * tile), (3 * tile, 3 * tile), (6 * tile, 2 * tile))
    return [(3, cuts[k], ORDERS[k]) for k in range(3)] + [(mat, (0, width), ORDERS[mat]) for mat in range(3)]


JOBS = range(6)
SMALL, LARGE = JOBS[:3], JOBS[3:]


def view(ref, lead, axes, sel, cols=None):
    mid = tuple(sel.get(a, slice(None)) for a in axes)
    last = (slice(None), pl.ds(*cols)) if cols is not None else ()
    return ref.at[lead + mid + last]


def half(axis, k):
    return {axis: pl.ds(2 * k, 2)}


def ring_places():
    me = {a: lax.axis_index(a) for a in CHIPS}
    near = {a: [lax.rem(me[a] + d, SIDE) for d in range(SIDE)] for a in CHIPS}
    return me, near


def enter(near, ring=True, partner=None):
    barrier = pltpu.get_barrier_semaphore()
    if ring:
        for axis in CHIPS:
            for d in (1, 3):
                pl.semaphore_signal(barrier, inc=1, device_id={axis: near[axis][d]}, device_id_type=MESH)
    if partner is not None:
        pl.semaphore_signal(barrier, inc=1, device_id={"c": partner}, device_id_type=MESH)
    pl.semaphore_wait(barrier, 6 * ring + (partner is not None))


class Sender:
    def __init__(self, near, send_sem, recv_sem):
        self.near, self.send_sem, self.recv_sem, self.open = near, send_sem, recv_sem, {}

    def put(self, key, src, dst, axis, step):
        copy = pltpu.make_async_remote_copy(
            src_ref=src, dst_ref=dst, send_sem=self.send_sem.at[key], recv_sem=self.recv_sem.at[key],
            device_id={axis: self.near[axis][step]}, device_id_type=MESH)
        copy.start()
        self.open[key] = copy

    def got(self, key):
        self.open[key].wait_recv()

    def close(self):
        for copy in self.open.values():
            copy.wait_send()


RING_SEMS = [pltpu.SemaphoreType.DMA((6, 3, 6)), pltpu.SemaphoreType.DMA((6, 3, 6))]


class Gather:
    def __init__(self, width, me, near, net, buf, lead=(), skip=0):
        self.me, self.near, self.net, self.buf, self.jobs = me, near, net, buf, jobs_of(width)
        self.lead, self.skip = lead, skip

    def block(self, job, fixed, more=None, ref=None, skip=None):
        mat, cols, order = self.jobs[job]
        skip = self.skip if skip is None else skip
        sel = {a: self.me[a] for a in order[:fixed]}
        sel.update(more or {})
        lead = self.lead if ref is None else ()
        return view(self.buf if ref is None else ref, lead + (mat,), [a for a in CHIPS if a not in order[:skip]], sel, cols)

    def push(self, job, phase, slot, d, part, step):
        order = self.jobs[job][2]
        axis = order[2 - phase]
        sel = {axis: self.near[axis][d]}
        if part is not None:
            sel.update(half(order[3 - phase], part))
        here = self.block(job, 2 - phase, sel)
        self.net.put((job, phase, slot), here, here, axis, step)

    def send(self, phase):
        halves = ((FULL, NEXT), (FULL, PREV)) if phase == 0 else ((0, NEXT), (1, PREV), (1, NEXT), (0, PREV))
        for job in JOBS:
            for slot, (part, step) in enumerate(halves):
                self.push(job, phase, slot, HERE, part, step)

    def forward(self, phase):
        for job in JOBS:
            self.net.got((job, phase, 0))
            if phase == 0:
                self.push(job, phase, 2, PREV, FULL, NEXT)
            else:
                self.push(job, phase, 4, PREV, 0, NEXT)
                self.net.got((job, phase, 1))
                self.push(job, phase, 5, NEXT, 1, PREV)

    def finish(self, phase):
        for job in JOBS:
            for slot in ((1, 2) if phase == 0 else (2, 3, 4, 5)):
                self.net.got((job, phase, slot))

    def through(self, phase):
        self.send(phase)
        self.forward(phase)
        self.finish(phase)

    def load(self, src, fixed, sems):
        return [pltpu.make_async_copy(self.block(job, fixed, ref=src, skip=fixed, more=None), self.block(job, fixed), sems.at[job])
                for job in JOBS]

    def store(self, out, d, sems):
        for job in JOBS:
            axis = self.jobs[job][2][0]
            sel = {axis: self.near[axis][d]}
            copy = pltpu.make_async_copy(self.block(job, 0, sel), self.block(job, 0, sel, ref=out), sems.at[job, d])
            copy.start()
            self.stores.append(copy)

    def last_sends(self, out, sems):
        self.stores = []
        self.send(2)
        self.store(out, HERE, sems)

    def close_out(self, out, sems):
        for slots, places in (((2, 3), (NEXT, PREV)), ((4, 5), (OPPOSITE,))):
            for job in JOBS:
                for slot in slots:
                    self.net.got((job, 2, slot))
            for d in places:
                self.store(out, d, sems)
        for copy in self.stores:
            copy.wait()


def column_places(rows, cols):
    src = lax.broadcasted_iota(jnp.int32, (rows, cols), 0)
    dst = lax.broadcasted_iota(jnp.int32, (rows, cols), 1)
    want = ((dst & 127) >> 4) * 64 + (dst >> 8) * 32 + ((dst >> 7) & 1) * 16 + (dst & 15)
    return jnp.where(src == want, 1.0, 0.0).astype(BF16)


def open_kernel(width, up, down, x_ref, g_ref, x_out, g_out, packed_out, full_out, quarter_out, line_out_0, line_out_1,
                perm, pack, x_val, g_val, buf, quarter, lines, send_a, recv_a, send_b, recv_b, send_c, recv_c,
                loc_sem, pair_send, pair_recv, line_sem, quarter_sem, store_sem):
    me, near = ring_places()
    core = lax.axis_index("c")
    tokens = x_ref.shape[0]
    mine = pl.ds(pl.multiple_of(core * tokens, tokens), tokens)
    rows = pl.ds(pl.multiple_of(core * 8, 8), 8)
    local = [pltpu.make_async_copy(down, pack.at[:, 2:4], loc_sem.at[0]),
             pltpu.make_async_copy(x_ref, x_val.at[mine], loc_sem.at[1]),
             pltpu.make_async_copy(g_ref, g_val.at[mine], loc_sem.at[2])]
    for copy in local:
        copy.start()
    enter(near, True, 1 - core)
    places = column_places(512, 512)
    flat = up[...].reshape(24, 4 * width)
    for group in range(4 * width // 512):
        moved = lax.dot_general(flat[:, group * 512:(group + 1) * 512], places, (((1,), (0,)), ((), ())),
                                preferred_element_type=F32).astype(BF16)
        for k in range(4):
            perm[:, k // 2, k % 2, :, group * 128:(group + 1) * 128] = moved[:, k * 128:(k + 1) * 128].reshape(3, 8, 128)
    pair = [pltpu.make_async_remote_copy(src_ref=src, dst_ref=dst, send_sem=pair_send.at[k], recv_sem=pair_recv.at[k],
                                         device_id={"c": 1 - core}, device_id_type=MESH)
            for k, (src, dst) in enumerate(((perm.at[:, 1 - core], pack.at[:, 0:2, rows]),
                                            (x_ref, x_val.at[mine]), (g_ref, g_val.at[mine])))]
    for copy in pair[1:]:
        copy.start()
    pair[0].start()
    own = pltpu.make_async_copy(perm.at[:, core], pack.at[:, 0:2, rows], loc_sem.at[3])
    own.start()
    local[0].wait()
    own.wait()
    pair[0].wait_recv()
    net_a, net_b, net_c = (Sender(near, *sems) for sems in ((send_a, recv_a), (send_b, recv_b), (send_c, recv_c)))
    ring = Gather(width, me, near, net_a, buf)
    line = [Gather(width, me, near, net, lines, (k,), 2) for k, net in ((0, net_b), (1, net_c))]
    ahead = Gather(width, me, near, net_b, quarter, (), 1)
    starts = [pltpu.make_async_copy(pack.at[0], view(buf, (slice(None),), CHIPS, me), line_sem.at[0, 0])]
    for k in range(2):
        for job, (mat, cols, order) in enumerate(jobs_of(width)):
            starts.append(pltpu.make_async_copy(pack.at[1 + k, mat, :, pl.ds(*cols)], line[k].block(job, 3), line_sem.at[1 + k, job]))
    for copy in starts:
        copy.start()
    save = pltpu.make_async_copy(pack.at[0], packed_out, loc_sem.at[4])
    save.start()
    for copy in starts:
        copy.wait()
    for part in [ring] + line:
        part.send(0)
    ring.forward(0)
    ring.finish(0)
    ring.send(1)
    for part in line:
        part.forward(0)
    ring.forward(1)
    ring.finish(1)
    ring.last_sends(full_out, store_sem)
    for part in line:
        part.finish(0)
    lines_save = [pltpu.make_async_copy(lines.at[k], out, loc_sem.at[9 + k]) for k, out in enumerate((line_out_0, line_out_1))]
    for copy in lines_save:
        copy.start()
    loads = ahead.load(lines.at[0], 2, quarter_sem)
    for copy in loads:
        copy.start()
    for copy in loads:
        copy.wait()
    ahead.send(1)
    for copy in local[1:]:
        copy.wait()
    for copy in pair[1:]:
        copy.wait_recv()
    outs = [pltpu.make_async_copy(x_val, x_out, loc_sem.at[6]), pltpu.make_async_copy(g_val, g_out, loc_sem.at[7])]
    for copy in outs:
        copy.start()
    ring.forward(2)
    ahead.forward(1)
    ahead.finish(1)
    outs.append(pltpu.make_async_copy(quarter, quarter_out, loc_sem.at[8]))
    outs[-1].start()
    ring.close_out(full_out, store_sem)
    for copy in outs + [save] + lines_save:
        copy.wait()
    for copy in pair:
        copy.wait_send()
    for net in (net_a, net_b, net_c):
        net.close()


def whole_of(width):
    return (4, SIDE, SIDE, SIDE, ROWS, width)


def open_call(up, down, x_loc, g_loc, call_id):
    tokens, width = x_loc.shape
    shape = lambda *dims: jax.ShapeDtypeStruct(dims, BF16)
    whole, quarter, line = whole_of(width), (4, SIDE, SIDE, ROWS, width), (4, SIDE, ROWS, width)
    vmem = lambda *dims: pltpu.VMEM(dims, BF16)
    sems = pltpu.SemaphoreType.DMA
    anywhere = pl.BlockSpec(memory_space=pl.ANY)
    return pl.pallas_call(
        functools.partial(open_kernel, width),
        out_shape=[shape(2 * tokens, width), shape(2 * tokens, width), shape(4, ROWS, width), shape(*whole), shape(*quarter), shape(*line), shape(*line)],
        in_specs=[pl.BlockSpec(memory_space=pltpu.VMEM)] + [anywhere] * 3,
        out_specs=[anywhere] * 7,
        scratch_shapes=[vmem(3, 2, 2, 8, width), vmem(3, 4, ROWS, width), vmem(2 * tokens, width), vmem(2 * tokens, width),
                        vmem(*whole), vmem(*quarter), vmem(2, *line)] + RING_SEMS * 3
        + [sems((11,)), sems((3,)), sems((3,)), sems((3, 6)), sems((6,)), sems((6, 4))],
        compiler_params=pltpu.CompilerParams(collective_id=call_id, has_side_effects=True, vmem_limit_bytes=VMEM_LIMIT),
        name="open",
    )(up, down.reshape(3, 2, ROWS, width), x_loc, g_loc)


def dot_nn(left, right):
    return lax.dot_general(left, right, (((1,), (0,)), ((), ())), preferred_element_type=F32)


def dot_nt(left, right):
    return lax.dot_general(left, right, (((1,), (1,)), ((), ())), preferred_element_type=F32)


def dot_tn(left, right):
    return lax.dot_general(left, right, (((0,), (0,)), ((), ())), preferred_element_type=F32)


def layer_kernel(forward, width, source, ahead, last_layer, *refs):
    refs = list(refs)
    take = lambda wanted: refs.pop(0) if wanted else None
    stream, weights, slope_in, begin, ahead_in = take(True), take(True), take(not forward), take(source), take(ahead)
    result, act_out, slope_out, next_out, ahead_out = take(True), take(True), take(forward), take(source), take(ahead)
    cur, mats, act, slope, part, got, pair_send, pair_recv, loc_sem, out_sem = refs[:10]
    tokens = cur.shape[0]
    tiles = tokens // TILE
    me, near = ring_places()
    core = lax.axis_index("c")
    partner = 1 - core
    loads = [pltpu.make_async_copy(stream, cur, loc_sem.at[0]), pltpu.make_async_copy(weights, mats, loc_sem.at[1])]
    if not forward:
        loads.append(pltpu.make_async_copy(slope_in, slope, loc_sem.at[2]))
    firsts = []
    if source:
        buf, send_sem, recv_sem, start_sem, store_sem = refs[10:15]
        net = Sender(near, send_sem, recv_sem)
        ring = Gather(width, me, near, net, buf)
        if source == "packed":
            firsts = [pltpu.make_async_copy(begin, view(buf, (slice(None),), CHIPS, me), start_sem.at[0])]
        else:
            firsts = ring.load(begin, 1 if source == "quarter" else 2, start_sem)
    if ahead:
        quarter, ahead_sem = refs[15:17]
        after = Gather(width, me, near, net, quarter, (), 1)
        firsts += after.load(ahead_in, 2, ahead_sem)
    for copy in firsts + loads:
        copy.start()
    enter(near, bool(source), partner)
    for copy in firsts:
        copy.wait()
    if ahead:
        after.send(1)
    if source == "packed":
        ring.through(0)
    if source in ("packed", "line"):
        ring.through(1)
    if source:
        ring.last_sends(next_out, store_sem)
    for copy in loads:
        copy.wait()

    def exchange(tile):
        rows = pl.ds(tile * TILE, TILE)
        return pltpu.make_async_remote_copy(
            src_ref=part.at[rows], dst_ref=got.at[rows], send_sem=pair_send.at[tile], recv_sem=pair_recv.at[tile],
            device_id={"c": partner}, device_id_type=MESH)

    def compute(tile, _):
        rows = pl.ds(pl.multiple_of(tile * TILE, TILE), TILE)
        left = cur[rows, :]
        for block in range(2):
            for cut in range(width // WIDE):
                cols = pl.ds(block * width + cut * WIDE, WIDE)
                if forward:
                    pre = dot_nn(left, mats[block * width:(block + 1) * width, cut * WIDE:(cut + 1) * WIDE])
                    act_val, slope_val = gelu_parts(pre)
                    act[rows, cols] = act_val.astype(BF16)
                    slope[rows, cols] = slope_val
                else:
                    low = (2 + block) * width + cut * WIDE
                    d_act = dot_nt(left, mats[low:low + WIDE, :])
                    act[rows, cols] = (d_act * slope[rows, cols]).astype(BF16)
        if forward:
            part[rows, :] = dot_nn(act[rows, :], mats[2 * width:, :])
        else:
            part[rows, :] = dot_nt(act[rows, :width], mats[:width, :]) + dot_nt(act[rows, width:], mats[width:2 * width, :])
        exchange(tile).start()
        return 0

    saves = []

    def save(k, low, high):
        rows = pl.ds(low * TILE, (high - low) * TILE)
        pairs = [(act, act_out)] + ([(slope, slope_out)] if forward else [])
        for n, (src, dst) in enumerate(pairs):
            saves.append(pltpu.make_async_copy(src.at[rows], dst.at[rows], out_sem.at[2 * k + n]))
            saves[-1].start()

    mid = tiles // 2
    lax.fori_loop(0, mid, compute, 0)
    save(0, 0, mid)
    if source:
        ring.forward(2)
    if ahead:
        after.forward(1)
    lax.fori_loop(mid, tiles, compute, 0)
    save(1, mid, tiles)
    for tile in range(tiles):
        exchange(tile).wait_recv()

    def total(rows):
        return (cur[rows, :].astype(F32) + (part[rows, :] + got[rows, :])).astype(BF16)

    if last_layer:
        for k in range(tiles // 2):
            rows = pl.ds(pl.multiple_of(core * (tokens // 2) + k * TILE, TILE), TILE)
            result[k * TILE:(k + 1) * TILE, :] = total(rows)
    else:
        for k in range(tiles):
            rows = pl.ds(k * TILE, TILE)
            result[rows, :] = total(rows)
    if ahead:
        after.finish(1)
        saves.append(pltpu.make_async_copy(quarter, ahead_out, out_sem.at[4]))
        saves[-1].start()
    if source:
        ring.close_out(next_out, store_sem)
        net.close()
    for copy in saves:
        copy.wait()
    for tile in range(tiles):
        exchange(tile).wait_send()


def layer_call(forward, stream, full, slope, call_id, source=None, begin=None, ahead=None, last_layer=False):
    tokens, width = stream.shape
    hidden = 2 * width
    shape = jax.ShapeDtypeStruct
    whole, quarter = whole_of(width), (4, SIDE, SIDE, ROWS, width)
    args = [stream, full.reshape(4 * width, width)] + ([] if forward else [slope])
    args += ([begin] if source else []) + ([] if ahead is None else [ahead])
    outs = [shape((tokens // 2 if last_layer else tokens, width), BF16), shape((tokens, hidden), BF16)]
    outs += [shape((tokens, hidden), F32)] if forward else []
    outs += ([shape(whole, BF16)] if source else []) + ([] if ahead is None else [shape(quarter, BF16)])
    tiles = tokens // TILE
    sems = pltpu.SemaphoreType.DMA
    scratch = [pltpu.VMEM((tokens, width), BF16), pltpu.VMEM((4 * width, width), BF16),
               pltpu.VMEM((tokens, hidden), BF16), pltpu.VMEM((tokens, hidden), F32),
               pltpu.VMEM((tokens, width), F32), pltpu.VMEM((tokens, width), F32),
               sems((tiles,)), sems((tiles,)), sems((4,)), sems((5,))]
    if source:
        scratch += [pltpu.VMEM(whole, BF16)] + RING_SEMS + [sems((6,)), sems((6, 4))]
    if ahead is not None:
        scratch += [pltpu.VMEM(quarter, BF16), sems((6,))]
    return pl.pallas_call(
        functools.partial(layer_kernel, forward, width, source, ahead is not None, last_layer),
        out_shape=outs,
        in_specs=[pl.BlockSpec(memory_space=pl.ANY)] * len(args),
        out_specs=[pl.BlockSpec(memory_space=pltpu.VMEM)] + [pl.BlockSpec(memory_space=pl.ANY)] * (len(outs) - 1),
        scratch_shapes=scratch,
        compiler_params=pltpu.CompilerParams(collective_id=call_id, has_side_effects=True, vmem_limit_bytes=VMEM_LIMIT),
        cost_estimate=pl.CostEstimate(flops=8 * tokens * hidden * width, bytes_accessed=40 << 20, transcendentals=0),
        name="forward_layer" if forward else "backward_layer",
    )(*args)


def add_into(dst, terms, lead):
    if not lead:
        dst[...] = sum((term[...] for term in terms), dst[...])
        return

    def step(k, _):
        add_into(dst.at[k], [term.at[k] for term in terms], lead[1:])
        return 0

    lax.fori_loop(0, lead[0], step, 0)


class RingSum:
    def __init__(self, width, me, near, buf, recv, send_sem, recv_sem):
        self.me, self.near, self.buf, self.recv, self.jobs = me, near, buf, recv, jobs_of(width)
        self.net = Sender(near, send_sem, recv_sem)

    def here(self, job, phase, d, part=None):
        mat, cols, order = self.jobs[job]
        sel = {a: self.me[a] for a in order[:phase]}
        sel[order[phase]] = self.near[order[phase]][d]
        if part is not None:
            sel.update(half(order[phase + 1], part))
        return view(self.buf, (mat,), CHIPS, sel, cols)

    def there(self, job, phase, slot, part=None):
        order = self.jobs[job][2]
        left = [a for a in CHIPS if a not in order[:phase + 1]]
        return view(self.recv[3 * job + phase], (slot,), left, {} if part is None else half(order[phase + 1], part))

    def lead(self, job, phase, part=None):
        order = self.jobs[job][2]
        return [2 if part is not None and a == order[phase + 1] else SIDE for a in CHIPS if a not in order[:phase + 1]]

    def push(self, job, phase, slot, d, part, to_slot, step):
        self.net.put((job, phase, slot), self.here(job, phase, d, part), self.there(job, phase, to_slot, part),
                     self.jobs[job][2][phase], step)

    def send(self, job, phase):
        if phase == 2:
            pieces = ((0, OPPOSITE, FULL, 0, NEXT), (3, PREV, FULL, 2, PREV))
        else:
            pieces = ((0, OPPOSITE, 0, 0, NEXT), (1, OPPOSITE, 1, 0, PREV), (2, NEXT, 1, 1, NEXT), (3, PREV, 0, 2, PREV))
        for slot, d, part, to_slot, step in pieces:
            self.push(job, phase, slot, d, part, to_slot, step)

    def pass_on(self, job, phase, arrived, slot, d, part, to_slot):
        self.net.got((job, phase, arrived))
        add_into(self.here(job, phase, d, part), [self.there(job, phase, 0, part)], self.lead(job, phase, part))
        self.push(job, phase, slot, d, part, to_slot, d)

    def mid(self, job, phase):
        if phase == 2:
            self.pass_on(job, phase, 0, 2, NEXT, FULL, 1)
        else:
            self.pass_on(job, phase, 0, 4, NEXT, 0, 1)
            self.pass_on(job, phase, 1, 5, PREV, 1, 2)

    def finish(self, job, phase):
        for slot in ((2, 3) if phase == 2 else (2, 3, 4, 5)):
            self.net.got((job, phase, slot))
        add_into(self.here(job, phase, HERE), [self.there(job, phase, slot) for slot in (1, 2)], self.lead(job, phase))


def recv_blocks(width):
    blocks = []
    for mat, cols, order in jobs_of(width):
        blocks += [pltpu.VMEM((3,) + (SIDE,) * (2 - phase) + (ROWS, cols[1]), F32) for phase in range(3)]
    return blocks


def sum_kernel(width, x_ref, act_ref, d_pre_ref, g_ref, up_out, down_out, x_val, act_val, d_pre, g_val, buf, *rest):
    send_sem, recv_sem, loc_sem, theirs, wide, pair_send, pair_recv = rest[18:]
    me, near = ring_places()
    core = lax.axis_index("c")
    ring = RingSum(width, me, near, buf, rest[:18], send_sem, recv_sem)
    upper, lower = pl.ds(0, width), pl.ds(width, width)
    loads = [pltpu.make_async_copy(src, dst, loc_sem.at[k]) for k, (src, dst) in enumerate(
        ((g_ref, g_val), (act_ref.at[:, lower], act_val.at[:, lower]), (act_ref.at[:, upper], act_val.at[:, upper]),
         (x_ref, x_val), (d_pre_ref, d_pre)))]
    for copy in loads:
        copy.start()
    enter(near, True, 1 - core)

    def grad(mat):
        def slab(z, _):
            if mat < 2:
                cols = pl.ds(pl.multiple_of(z * (width // SIDE), width // SIDE), width // SIDE)
                val = dot_tn(x_val[:, cols], d_pre[:, mat * width:(mat + 1) * width])
            else:
                cols = pl.ds(pl.multiple_of((mat - 2) * width + z * (width // SIDE), width // SIDE), width // SIDE)
                val = dot_tn(act_val[:, cols], g_val[...])
            buf[mat, z] = val.reshape(SIDE, SIDE, ROWS, width)
            return 0

        lax.fori_loop(0, SIDE, slab, 0)

    for copy in loads[:2]:
        copy.wait()
    grad(3)
    for job in SMALL:
        ring.send(job, 0)
    for copy in loads[2:]:
        copy.wait()
    for mat in (2, 0, 1):
        grad(mat)
        ring.send(LARGE[mat], 0)
        if mat == 0:
            for job in SMALL:
                ring.mid(job, 0)
    for job in LARGE:
        ring.mid(job, 0)
    for phase in range(3):
        for group in (SMALL, LARGE):
            for job in group:
                ring.finish(job, phase)
                if phase < 2:
                    ring.send(job, phase + 1)
        if phase < 2:
            for group in (SMALL, LARGE):
                for job in group:
                    ring.mid(job, phase + 1)
    own = [view(buf, (mat,), CHIPS, me) for mat in range(4)]
    pair = [pltpu.make_async_remote_copy(
        src_ref=own[mat].at[pl.ds(pl.multiple_of(8 * (1 - core), 8), 8)], dst_ref=theirs.at[mat], send_sem=pair_send.at[mat],
        recv_sem=pair_recv.at[mat], device_id={"c": 1 - core}, device_id_type=MESH) for mat in range(2)]
    for copy in pair:
        copy.start()
    for mat in (2, 3):
        down_out[(mat - 2) * ROWS:(mat - 1) * ROWS, :] = own[mat][...]
    places = column_places(512, 512)
    for copy in pair:
        copy.wait_recv()
    kept = pl.ds(pl.multiple_of(8 * core, 8), 8)
    for mat in range(2):
        first, second = own[mat][kept, :], theirs[mat]
        low, high = jnp.where(core == 0, first, second), jnp.where(core == 0, second, first)
        for group in range(width // 128):
            rows, cols = slice(8 * group, 8 * group + 8), slice(128 * group, 128 * group + 128)
            wide[rows, 128 * mat:128 * mat + 128] = low[:, cols]
            wide[rows, 256 + 128 * mat:384 + 128 * mat] = high[:, cols]
    rest_val = wide[...]
    total = None
    for _ in range(3):
        piece = rest_val.astype(BF16)
        rest_val = rest_val - piece.astype(F32)
        term = dot_nt(piece, places)
        total = term if total is None else total + term
    for group in range(width // 128):
        up_out[:, 512 * group:512 * group + 512] = total[8 * group:8 * group + 8, :]
    for copy in pair:
        copy.wait_send()
    ring.net.close()


def scatter_sum(x_in, act, d_pre, g_in, call_id):
    tokens, width = x_in.shape
    return pl.pallas_call(
        functools.partial(sum_kernel, width),
        out_shape=[jax.ShapeDtypeStruct((8, 4 * width), F32), jax.ShapeDtypeStruct((2 * ROWS, width), F32)],
        in_specs=[pl.BlockSpec(memory_space=pl.ANY)] * 4,
        out_specs=[pl.BlockSpec(memory_space=pltpu.VMEM)] * 2,
        scratch_shapes=[pltpu.VMEM((tokens, width), BF16), pltpu.VMEM((tokens, 2 * width), BF16),
                        pltpu.VMEM((tokens, 2 * width), BF16), pltpu.VMEM((tokens, width), BF16),
                        pltpu.VMEM((4, SIDE, SIDE, SIDE, ROWS, width), F32)] + recv_blocks(width)
        + RING_SEMS + [pltpu.SemaphoreType.DMA((5,)), pltpu.VMEM((2, 8, width), F32), pltpu.VMEM((8 * (width // 128), 512), F32),
                       pltpu.SemaphoreType.DMA((2,)), pltpu.SemaphoreType.DMA((2,))],
        compiler_params=pltpu.CompilerParams(collective_id=call_id, has_side_effects=True, vmem_limit_bytes=VMEM_LIMIT),
        cost_estimate=pl.CostEstimate(flops=8 * tokens * width * width, bytes_accessed=12 << 20, transcendentals=0),
        name="scatter_sum",
    )(x_in, act, d_pre, g_in)


def solution(mesh):
    grid = Mesh(mesh.devices.reshape(SIDE, SIDE, SIDE, 2), ALL)
    tok_spec = P(ALL, None)
    weight_spec = P(None, ALL, None)

    def device_step(x_loc, up_loc, down_loc, g_loc):
        x_0, g_3, packed, full, quarter_1, line_1, line_2 = open_call(up_loc, down_loc, x_loc, g_loc, 0)
        x_1, act_0, slope_0, full, quarter_2 = layer_call(True, x_0, full, None, 1, "quarter", quarter_1, line_2)
        x_2, act_1, slope_1, full = layer_call(True, x_1, full, None, 2, "quarter", quarter_2)
        y_out, act_2, slope_2, full = layer_call(True, x_2, full, None, 3, "line", line_2, last_layer=True)
        g_2, d_pre_2, full = layer_call(False, g_3, full, slope_2, 4, "line", line_1)
        sum_2 = scatter_sum(x_2, act_2, d_pre_2, g_3, 5)
        g_1, d_pre_1, full = layer_call(False, g_2, full, slope_1, 6, "packed", packed)
        sum_1 = scatter_sum(x_1, act_1, d_pre_1, g_2, 7)
        grad_in, d_pre_0 = layer_call(False, g_1, full, slope_0, 8, last_layer=True)
        sum_0 = scatter_sum(x_0, act_0, d_pre_0, g_1, 9)
        grad_up, grad_down = (jnp.stack(parts) for parts in zip(sum_0, sum_1, sum_2, strict=True))
        return y_out, grad_in, grad_up, grad_down

    return jax.shard_map(device_step, mesh=grid, in_specs=(tok_spec, weight_spec, weight_spec, tok_spec),
                         out_specs=(tok_spec, tok_spec, weight_spec, weight_spec), check_vma=False)
```

time: 588 us -> 544 us (0.925)
  local copies, waits for them, and re-layouts: 29.7 us -> 3.25 us
  Pallas kernels: 538 us -> 528 us
    reshape x5 -> x0, local copies, waits for them, and re-layouts: 14.5 us -> none  [the longest x1 5.54 us: unpack_up_grad(): return both.transpose(1, 3, 4, 0, 2, 5).reshape(layers, 8, 4096)]
    pallas_call x10, Pallas kernels: 538 us -> 528 us  [the longest x3 237 us: scatter_sum(): pl.pallas_call(functools.partial(sum_kernel, width), out_shape=[jax.Shape...]
    dynamic_slice x6 -> x0, local copies, waits for them, and re-layouts: 9.95 us -> none  [the longest x2 2.34 us: unpack_up_grad(): mine = lax.dynamic_index_in_dim(rows, core, 2, keepdims=False)]
  transfers between devices with their start and end apart: 4 -> 0, of which waited for: 0 -> 0; matrix products, arithmetic and copies ran while one was open for 3% -> 0% of each run, Pallas kernels for 8% -> 0%
where the time goes in v3:
time: 544 us; the launch traced here: 536 us
  Pallas kernels  528 us (97%)
    pallas_call x3, Pallas kernels, scatter_sum(): pl.pallas_call(functools.partial(sum_kernel, width), out_shape=[jax.Shape...  237 us
    pallas_call x6, Pallas kernels, layer_call(): pl.pallas_call(functools.partial(layer_kernel, forward, width, source, ah...  221 us
    pallas_call x1, Pallas kernels, open_call(): pl.pallas_call(functools.partial(open_kernel, width), out_shape=[shape(2...  69.5 us

profile of v3, /device:TPU:1, one launch (start us, length us, event | category | flops | bytes accessed | tf_op | source)
XLA Modules:
  0.0 535.8 jit_solution(5088653904565111968)
XLA Ops:
  0.6 69.5 %open.1 = (bf16[1024,1024]{1,0:T(8,128)(2,1)}, bf16[1024,1024]{1,0:T(8,128)(2,1)}, bf16[4,16,1024]{2,1,0:T(8,128)(2,1)}, bf16[4,4,4,4,16,1024]{5,4,3,2,1,0:T(8,1...) custom-call(bf16[3,8,4096]{2,1,0:T(8,128)(2,1)} %up.1, ...), custom_call_target="tpu_custom_call" | custom-call | tf_op jit(solution)/shard_map/open/pallas_call | solution.py:275
  70.2 39.4 %forward_layer.3 = (bf16[1024,1024]{1,0:T(8,128)(2,1)}, bf16[1024,2048]{1,0:T(8,128)(2,1)}, f32[1024,2048]{1,0:T(8,128)}, bf16[4,4,4,4,16,1024]{5,4,3,2,1,0:T(8,128)(2,1)}, bf16[4,4,4,16,1024]{4,3,2,1,0:T(8,128)(2,1)}) custom-call(bf16[1024,1024]{1,0:T(8,128)(2,1)} %get-tuple-element.38.refs_0_.x_ref, bf16[4096,1024]{1,0:T(8,128)(2,1)} %bitcast.20, ...), custom_call_target="tpu_custom_call" | custom-call | flops 17179869184 | bytes 41943040 | tf_op jit(solution)/shard_map/forward_layer/pallas_call | solution.py:436
  109.6 31.7 %forward_layer.4 = (bf16[1024,1024]{1,0:T(8,128)(2,1)}, bf16[1024,2048]{1,0:T(8,128)(2,1)}, f32[1024,2048]{1,0:T(8,128)}, bf16[4,4,4,4,16,1024]{5,4,3,2,1,0:T(8,128)(2,1)}) custom-call(bf16[1024,1024]{1,0:T(8,128)(2,1)} %get-tuple-element.42.refs_0_.x_ref, bf16[4096,1024]{1,0:T(8,128)(2,1)} %bitcast.23, bf16[4,4,4,16,1024]{4,3,2,1,0:T(8,128)(2,1)} %get-tuple-element.44.refs_2_), custom_call_target="tpu_custom_call" | custom-call | flops 17179869184 | bytes 41943040 | tf_op jit(solution)/shard_map/forward_layer/pallas_call | solution.py:436
  141.3 40.6 %forward_layer.5 = (bf16[512,1024]{1,0:T(8,128)(2,1)}, bf16[1024,2048]{1,0:T(8,128)(2,1)}, f32[1024,2048]{1,0:T(8,128)}, bf16[4,4,4,4,16,1024]{5,4,3,2,1,0:T(8,128)(2,1)}) custom-call(bf16[1024,1024]{1,0:T(8,128)(2,1)} %get-tuple-element.45.refs_0_.x_ref, bf16[4096,1024]{1,0:T(8,128)(2,1)} %bitcast.24, bf16[4,4,16,1024]{3,2,1,0:T(8,128)(2,1)} %get-tuple-element.41.refs_3_.refs_2_), custom_call_target="tpu_custom_call" | custom-call | flops 17179869184 | bytes 41943040 | tf_op jit(solution)/shard_map/forward_layer/pallas_call | solution.py:436
  181.9 41.6 %backward_layer.3 = (bf16[1024,1024]{1,0:T(8,128)(2,1)}, bf16[1024,2048]{1,0:T(8,128)(2,1)}, bf16[4,4,4,4,16,1024]{5,4,3,2,1,0:T(8,128)(2,1)}) custom-call(bf16[1024,1024]{1,0:T(8,128)(2,1)} %get-tuple-element.48.refs_0_.g_ref, bf16[4096,1024]{1,0:T(8,128)(2,1)} %bitcast.25, f32[1024,2048]{1,0:T(8,128)} %get-tuple-element.50.refs_2_, ...), custom_call_target="tpu_custom_call" | custom-call | flops 17179869184 | bytes 41943040 | tf_op jit(solution)/shard_map/backward_layer/pallas_call | solution.py:436
  223.6 79.1 %scatter_sum.5 = (f32[8,4096]{1,0:T(8,128)}, f32[32,1024]{1,0:T(8,128)}) custom-call(bf16[1024,1024]{1,0:T(8,128)(2,1)} %get-tuple-element.45.refs_0_.x_ref, bf16[1024,2048]{1,0:T(8,128)(2,1)} %get-tuple-element.66.act_ref, bf16[1024,2048]{1,0:T(8,128)(2,1)} %get-tuple-element.67.d_pre_ref, bf16[1024,1024]{1,0:T(8,128)(2,1)} %get-tuple-element.48.refs_0_.g_ref), custom_call_target="tpu_custom_call" | custom-call | flops 8589934592 | bytes 12582912 | tf_op jit(solution)/shard_map/scatter_sum/pallas_call | solution.py:605
  302.7 48.7 %backward_layer.4 = (bf16[1024,1024]{1,0:T(8,128)(2,1)}, bf16[1024,2048]{1,0:T(8,128)(2,1)}, bf16[4,4,4,4,16,1024]{5,4,3,2,1,0:T(8,128)(2,1)}) custom-call(bf16[1024,1024]{1,0:T(8,128)(2,1)} %get-tuple-element.52.refs_0_.g_ref, bf16[4096,1024]{1,0:T(8,128)(2,1)} %bitcast.21, f32[1024,2048]{1,0:T(8,128)} %get-tuple-element.54.refs_2_, ...), custom_call_target="tpu_custom_call" | custom-call | flops 17179869184 | bytes 41943040 | tf_op jit(solution)/shard_map/backward_layer/pallas_call | solution.py:436
  351.4 79.6 %scatter_sum.4 = (f32[8,4096]{1,0:T(8,128)}, f32[32,1024]{1,0:T(8,128)}) custom-call(bf16[1024,1024]{1,0:T(8,128)(2,1)} %get-tuple-element.42.refs_0_.x_ref, bf16[1024,2048]{1,0:T(8,128)(2,1)} %get-tuple-element.63.act_ref, bf16[1024,2048]{1,0:T(8,128)(2,1)} %get-tuple-element.64.d_pre_ref, bf16[1024,1024]{1,0:T(8,128)(2,1)} %get-tuple-element.52.refs_0_.g_ref), custom_call_target="tpu_custom_call" | custom-call | flops 8589934592 | bytes 12582912 | tf_op jit(solution)/shard_map/scatter_sum/pallas_call | solution.py:605
  431.0 19.3 %backward_layer.5 = (bf16[512,1024]{1,0:T(8,128)(2,1)}, bf16[1024,2048]{1,0:T(8,128)(2,1)}) custom-call(bf16[1024,1024]{1,0:T(8,128)(2,1)} %get-tuple-element.56.refs_0_.g_ref, bf16[4096,1024]{1,0:T(8,128)(2,1)} %bitcast.22, f32[1024,2048]{1,0:T(8,128)} %get-tuple-element.58.refs_2_), custom_call_target="tpu_custom_call" | custom-call | flops 17179869184 | bytes 41943040 | tf_op jit(solution)/shard_map/backward_layer/pallas_call | solution.py:436
  450.3 0.0 copy-start.2
  450.4 0.0 copy-start.4
  450.4 0.0 copy-start.1
  450.4 0.0 copy-start.3
  450.4 78.6 %scatter_sum.3 = (f32[8,4096]{1,0:T(8,128)}, f32[32,1024]{1,0:T(8,128)}) custom-call(bf16[1024,1024]{1,0:T(8,128)(2,1)} %get-tuple-element.38.refs_0_.x_ref, bf16[1024,2048]{1,0:T(8,128)(2,1)} %get-tuple-element.60.act_ref, bf16[1024,2048]{1,0:T(8,128)(2,1)} %get-tuple-element.61.d_pre_ref, bf16[1024,1024]{1,0:T(8,128)(2,1)} %get-tuple-element.56.refs_0_.g_ref), custom_call_target="tpu_custom_call" | custom-call | flops 8589934592 | bytes 12582912 | tf_op jit(solution)/shard_map/scatter_sum/pallas_call | solution.py:605
  528.9 0.0 copy-start
  529.0 0.0 copy-done.2
  529.0 0.0 copy-done.4
  529.0 1.8 pad_maximum_fusion
  530.7 0.0 copy-done.1
  530.7 0.0 copy-done.3
  530.7 1.7 pad_maximum_fusion.1
  532.4 2.3 copy.10
  534.7 0.0 copy-done
  534.7 1.0 copy.11
Async XLA Ops:
  450.3 78.6 %copy-start.2 = (f32[8,4096]{1,0:T(8,128)S(1)}, f32[8,4096]{1,0:T(8,128)}, u32[]{:S(2)}) copy-start(f32[8,4096]{1,0:T(8,128)} %get-tuple-element.68) | copy-start | bytes 393220
  450.4 78.6 %copy-start.4 = (f32[8,4096]{1,0:T(8,128)S(1)}, f32[8,4096]{1,0:T(8,128)}, u32[]{:S(2)}) copy-start(f32[8,4096]{1,0:T(8,128)} %get-tuple-element.65) | copy-start | bytes 393220
  450.4 80.4 %copy-start.1 = (f32[32,1024]{1,0:T(8,128)S(1)}, f32[32,1024]{1,0:T(8,128)}, u32[]{:S(2)}) copy-start(f32[32,1024]{1,0:T(8,128)} %get-tuple-element.71) | copy-start | bytes 393220
  450.4 80.4 %copy-start.3 = (f32[32,1024]{1,0:T(8,128)S(1)}, f32[32,1024]{1,0:T(8,128)}, u32[]{:S(2)}) copy-start(f32[32,1024]{1,0:T(8,128)} %get-tuple-element.70) | copy-start | bytes 393220
  528.9 5.7 %copy-start = (bf16[512,1024]{1,0:T(8,128)(2,1)S(1)}, bf16[512,1024]{1,0:T(8,128)(2,1)}, u32[]{:S(2)}) copy-start(bf16[512,1024]{1,0:T(8,128)(2,1)} %get-tuple-element.77) | copy-start | bytes 3145732

commit v4 on v3

--- a/solution.py
+++ b/solution.py
@@ -297,11 +297,14 @@
     return lax.dot_general(left, right, (((0,), (0,)), ((), ())), preferred_element_type=F32)
 
 
-def layer_kernel(forward, width, source, ahead, last_layer, *refs):
+def layer_kernel(forward, width, source, ahead, pre, last_layer, *refs):
     refs = list(refs)
     take = lambda wanted: refs.pop(0) if wanted else None
-    stream, weights, slope_in, begin, ahead_in = take(True), take(True), take(not forward), take(source), take(ahead)
-    result, act_out, slope_out, next_out, ahead_out = take(True), take(True), take(forward), take(source), take(ahead)
+    stream, weights, slope_in, act_in = take(True), take(True), take(not forward), take(not forward)
+    begin, ahead_in, pre_in = take(source), take(ahead), take(pre)
+    result, act_out, slope_out, grad_out = take(True), take(True), take(forward), take(not forward)
+    next_out, ahead_out, pre_out = take(source), take(ahead), take(pre)
+    act_low, grad_low = (refs.pop(), refs.pop()) if not forward else (None, None)
     cur, mats, act, slope, part, got, pair_send, pair_recv, loc_sem, out_sem = refs[:10]
     tokens = cur.shape[0]
     tiles = tokens // TILE
@@ -311,19 +314,22 @@
     loads = [pltpu.make_async_copy(stream, cur, loc_sem.at[0]), pltpu.make_async_copy(weights, mats, loc_sem.at[1])]
     if not forward:
         loads.append(pltpu.make_async_copy(slope_in, slope, loc_sem.at[2]))
+        loads.append(pltpu.make_async_copy(act_in.at[:, pl.ds(width, width)], act_low, loc_sem.at[3]))
     firsts = []
     if source:
         buf, send_sem, recv_sem, start_sem, store_sem = refs[10:15]
         net = Sender(near, send_sem, recv_sem)
         ring = Gather(width, me, near, net, buf)
-        if source == "packed":
-            firsts = [pltpu.make_async_copy(begin, view(buf, (slice(None),), CHIPS, me), start_sem.at[0])]
-        else:
-            firsts = ring.load(begin, 1 if source == "quarter" else 2, start_sem)
+        firsts = ring.load(begin, 1 if source == "quarter" else 2, start_sem)
     if ahead:
         quarter, ahead_sem = refs[15:17]
         after = Gather(width, me, near, net, quarter, (), 1)
         firsts += after.load(ahead_in, 2, ahead_sem)
+    if pre:
+        line, pre_sem = refs[15:17]
+        before = Gather(width, me, near, net, line, (), 2)
+        firsts += [pltpu.make_async_copy(pre_in.at[mat, :, pl.ds(*cols)], before.block(job, 3), pre_sem.at[job])
+                   for job, (mat, cols, order) in enumerate(before.jobs)]
     for copy in firsts + loads:
         copy.start()
     enter(near, bool(source), partner)
@@ -331,9 +337,9 @@
         copy.wait()
     if ahead:
         after.send(1)
-    if source == "packed":
-        ring.through(0)
-    if source in ("packed", "line"):
+    if pre:
+        before.send(0)
+    if source == "line":
         ring.through(1)
     if source:
         ring.last_sends(next_out, store_sem)
@@ -368,6 +374,12 @@
         exchange(tile).start()
         return 0
 
+    def low_slab(z, _):
+        slab = width // SIDE
+        val = dot_tn(act_low[:, pl.ds(pl.multiple_of(z * slab, slab), slab)], cur[...])
+        grad_low[z] = val.reshape(SIDE, SIDE, ROWS, width)
+        return 0
+
     saves = []
 
     def save(k, low, high):
@@ -384,6 +396,12 @@
         ring.forward(2)
     if ahead:
         after.forward(1)
+    if pre:
+        before.forward(0)
+    if not forward:
+        lax.fori_loop(0, SIDE, low_slab, 0)
+        saves.append(pltpu.make_async_copy(grad_low, grad_out, out_sem.at[1]))
+        saves[-1].start()
     lax.fori_loop(mid, tiles, compute, 0)
     save(1, mid, tiles)
     for tile in range(tiles):
@@ -404,6 +422,10 @@
         after.finish(1)
         saves.append(pltpu.make_async_copy(quarter, ahead_out, out_sem.at[4]))
         saves[-1].start()
+    if pre:
+        before.finish(0)
+        saves.append(pltpu.make_async_copy(line, pre_out, out_sem.at[4]))
+        saves[-1].start()
     if source:
         ring.close_out(next_out, store_sem)
         net.close()
@@ -413,16 +435,17 @@
         exchange(tile).wait_send()
 
 
-def layer_call(forward, stream, full, slope, call_id, source=None, begin=None, ahead=None, last_layer=False):
+def layer_call(forward, stream, full, kept, call_id, source=None, begin=None, ahead=None, pre=None, last_layer=False):
     tokens, width = stream.shape
     hidden = 2 * width
     shape = jax.ShapeDtypeStruct
     whole, quarter = whole_of(width), (4, SIDE, SIDE, ROWS, width)
-    args = [stream, full.reshape(4 * width, width)] + ([] if forward else [slope])
-    args += ([begin] if source else []) + ([] if ahead is None else [ahead])
+    args = [stream, full.reshape(4 * width, width)] + ([] if forward else list(kept))
+    args += [val for val in (begin, ahead, pre) if val is not None]
     outs = [shape((tokens // 2 if last_layer else tokens, width), BF16), shape((tokens, hidden), BF16)]
-    outs += [shape((tokens, hidden), F32)] if forward else []
+    outs += [shape((tokens, hidden), F32) if forward else shape(whole[1:], F32)]
     outs += ([shape(whole, BF16)] if source else []) + ([] if ahead is None else [shape(quarter, BF16)])
+    outs += [] if pre is None else [shape(quarter[1:], BF16)]
     tiles = tokens // TILE
     sems = pltpu.SemaphoreType.DMA
     scratch = [pltpu.VMEM((tokens, width), BF16), pltpu.VMEM((4 * width, width), BF16),
@@ -433,8 +456,12 @@
         scratch += [pltpu.VMEM(whole, BF16)] + RING_SEMS + [sems((6,)), sems((6, 4))]
     if ahead is not None:
         scratch += [pltpu.VMEM(quarter, BF16), sems((6,))]
+    if pre is not None:
+        scratch += [pltpu.VMEM(quarter[1:], BF16), sems((6,))]
+    if not forward:
+        scratch += [pltpu.VMEM(whole[1:], F32), pltpu.VMEM((tokens, width), BF16)]
     return pl.pallas_call(
-        functools.partial(layer_kernel, forward, width, source, ahead is not None, last_layer),
+        functools.partial(layer_kernel, forward, width, source, ahead is not None, pre is not None, last_layer),
         out_shape=outs,
         in_specs=[pl.BlockSpec(memory_space=pl.ANY)] * len(args),
         out_specs=[pl.BlockSpec(memory_space=pltpu.VMEM)] + [pl.BlockSpec(memory_space=pl.ANY)] * (len(outs) - 1),
@@ -516,15 +543,20 @@
     return blocks
 
 
-def sum_kernel(width, x_ref, act_ref, d_pre_ref, g_ref, up_out, down_out, x_val, act_val, d_pre, g_val, buf, *rest):
-    send_sem, recv_sem, loc_sem, theirs, wide, pair_send, pair_recv = rest[18:]
+def sum_kernel(width, x_ref, act_ref, d_pre_ref, g_ref, low_ref, up_out, down_out, x_val, act_val, d_pre, g_val, buf, *rest):
+    send_sem, recv_sem, loc_sem, theirs, wide, pair_send, pair_recv, low_sem = rest[18:]
     me, near = ring_places()
     core = lax.axis_index("c")
     ring = RingSum(width, me, near, buf, rest[:18], send_sem, recv_sem)
-    upper, lower = pl.ds(0, width), pl.ds(width, width)
+    low = {}
+    for d in (OPPOSITE, NEXT, PREV, HERE):
+        for job in SMALL:
+            mat, cols, order = ring.jobs[job]
+            src = view(low_ref, (), CHIPS, {order[0]: near[order[0]][d]}, cols)
+            low[job, d] = pltpu.make_async_copy(src, ring.here(job, 0, d), low_sem.at[job, d])
+            low[job, d].start()
     loads = [pltpu.make_async_copy(src, dst, loc_sem.at[k]) for k, (src, dst) in enumerate(
-        ((g_ref, g_val), (act_ref.at[:, lower], act_val.at[:, lower]), (act_ref.at[:, upper], act_val.at[:, upper]),
-         (x_ref, x_val), (d_pre_ref, d_pre)))]
+        ((g_ref, g_val), (act_ref.at[:, pl.ds(0, width)], act_val), (x_ref, x_val), (d_pre_ref, d_pre)))]
     for copy in loads:
         copy.start()
     enter(near, True, 1 - core)
@@ -535,19 +567,18 @@
                 cols = pl.ds(pl.multiple_of(z * (width // SIDE), width // SIDE), width // SIDE)
                 val = dot_tn(x_val[:, cols], d_pre[:, mat * width:(mat + 1) * width])
             else:
-                cols = pl.ds(pl.multiple_of((mat - 2) * width + z * (width // SIDE), width // SIDE), width // SIDE)
+                cols = pl.ds(pl.multiple_of(z * (width // SIDE), width // SIDE), width // SIDE)
                 val = dot_tn(act_val[:, cols], g_val[...])
             buf[mat, z] = val.reshape(SIDE, SIDE, ROWS, width)
             return 0
 
         lax.fori_loop(0, SIDE, slab, 0)
 
-    for copy in loads[:2]:
-        copy.wait()
-    grad(3)
     for job in SMALL:
+        for d in (OPPOSITE, NEXT, PREV):
+            low[job, d].wait()
         ring.send(job, 0)
-    for copy in loads[2:]:
+    for copy in loads:
         copy.wait()
     for mat in (2, 0, 1):
         grad(mat)
@@ -557,6 +588,8 @@
                 ring.mid(job, 0)
     for job in LARGE:
         ring.mid(job, 0)
+    for job in SMALL:
+        low[job, HERE].wait()
     for phase in range(3):
         for group in (SMALL, LARGE):
             for job in group:
@@ -600,22 +633,22 @@
     ring.net.close()
 
 
-def scatter_sum(x_in, act, d_pre, g_in, call_id):
+def scatter_sum(x_in, act, d_pre, g_in, low, call_id):
     tokens, width = x_in.shape
     return pl.pallas_call(
         functools.partial(sum_kernel, width),
         out_shape=[jax.ShapeDtypeStruct((8, 4 * width), F32), jax.ShapeDtypeStruct((2 * ROWS, width), F32)],
-        in_specs=[pl.BlockSpec(memory_space=pl.ANY)] * 4,
+        in_specs=[pl.BlockSpec(memory_space=pl.ANY)] * 5,
         out_specs=[pl.BlockSpec(memory_space=pltpu.VMEM)] * 2,
-        scratch_shapes=[pltpu.VMEM((tokens, width), BF16), pltpu.VMEM((tokens, 2 * width), BF16),
+        scratch_shapes=[pltpu.VMEM((tokens, width), BF16), pltpu.VMEM((tokens, width), BF16),
                         pltpu.VMEM((tokens, 2 * width), BF16), pltpu.VMEM((tokens, width), BF16),
                         pltpu.VMEM((4, SIDE, SIDE, SIDE, ROWS, width), F32)] + recv_blocks(width)
         + RING_SEMS + [pltpu.SemaphoreType.DMA((5,)), pltpu.VMEM((2, 8, width), F32), pltpu.VMEM((8 * (width // 128), 512), F32),
-                       pltpu.SemaphoreType.DMA((2,)), pltpu.SemaphoreType.DMA((2,))],
+                       pltpu.SemaphoreType.DMA((2,)), pltpu.SemaphoreType.DMA((2,)), pltpu.SemaphoreType.DMA((3, 4))],
         compiler_params=pltpu.CompilerParams(collective_id=call_id, has_side_effects=True, vmem_limit_bytes=VMEM_LIMIT),
         cost_estimate=pl.CostEstimate(flops=8 * tokens * width * width, bytes_accessed=12 << 20, transcendentals=0),
         name="scatter_sum",
-    )(x_in, act, d_pre, g_in)
+    )(x_in, act, d_pre, g_in, low)
 
 
 def solution(mesh):
@@ -628,12 +661,12 @@
         x_1, act_0, slope_0, full, quarter_2 = layer_call(True, x_0, full, None, 1, "quarter", quarter_1, line_2)
         x_2, act_1, slope_1, full = layer_call(True, x_1, full, None, 2, "quarter", quarter_2)
         y_out, act_2, slope_2, full = layer_call(True, x_2, full, None, 3, "line", line_2, last_layer=True)
-        g_2, d_pre_2, full = layer_call(False, g_3, full, slope_2, 4, "line", line_1)
-        sum_2 = scatter_sum(x_2, act_2, d_pre_2, g_3, 5)
-        g_1, d_pre_1, full = layer_call(False, g_2, full, slope_1, 6, "packed", packed)
-        sum_1 = scatter_sum(x_1, act_1, d_pre_1, g_2, 7)
-        grad_in, d_pre_0 = layer_call(False, g_1, full, slope_0, 8, last_layer=True)
-        sum_0 = scatter_sum(x_0, act_0, d_pre_0, g_1, 9)
+        g_2, d_pre_2, low_2, full, line_0 = layer_call(False, g_3, full, (slope_2, act_2), 4, "line", line_1, pre=packed)
+        sum_2 = scatter_sum(x_2, act_2, d_pre_2, g_3, low_2, 5)
+        g_1, d_pre_1, low_1, full = layer_call(False, g_2, full, (slope_1, act_1), 6, "line", line_0)
+        sum_1 = scatter_sum(x_1, act_1, d_pre_1, g_2, low_1, 7)
+        grad_in, d_pre_0, low_0 = layer_call(False, g_1, full, (slope_0, act_0), 8, last_layer=True)
+        sum_0 = scatter_sum(x_0, act_0, d_pre_0, g_1, low_0, 9)
         grad_up, grad_down = (jnp.stack(parts) for parts in zip(sum_0, sum_1, sum_2, strict=True))
         return y_out, grad_in, grad_up, grad_down
 

time: 544 us -> 543 us (level)
    pallas_call x3, Pallas kernels: 237 us -> 230 us  [scatter_sum(): pl.pallas_call(functools.partial(sum_kernel, width), out_shape=[jax.Shape...]
where the time goes in v4:
time: 543 us; the launch traced here: 534 us
  Pallas kernels  526 us (97%)
    pallas_call x3, Pallas kernels, scatter_sum(): pl.pallas_call(functools.partial(sum_kernel, width), out_shape=[jax.Shape...  230 us
    pallas_call x6, Pallas kernels, layer_call(): pl.pallas_call(functools.partial(layer_kernel, forward, width, source, ah...  227 us
    pallas_call x1, Pallas kernels, open_call(): pl.pallas_call(functools.partial(open_kernel, width), out_shape=[shape(2...  69.5 us

profile of v4, /device:TPU:1, one launch (start us, length us, event | category | flops | bytes accessed | tf_op | source)
XLA Modules:
  0.0 534.4 jit_solution(11857802471102769793)
XLA Ops:
  0.6 69.5 %open.1 = (bf16[1024,1024]{1,0:T(8,128)(2,1)}, bf16[1024,1024]{1,0:T(8,128)(2,1)}, bf16[4,16,1024]{2,1,0:T(8,128)(2,1)}, bf16[4,4,4,4,16,1024]{5,4,3,2,1,0:T(8,1...) custom-call(bf16[3,8,4096]{2,1,0:T(8,128)(2,1)} %up.1, ...), custom_call_target="tpu_custom_call" | custom-call | tf_op jit(solution)/shard_map/open/pallas_call | solution.py:275
  70.2 39.4 %forward_layer.3 = (bf16[1024,1024]{1,0:T(8,128)(2,1)}, bf16[1024,2048]{1,0:T(8,128)(2,1)}, f32[1024,2048]{1,0:T(8,128)}, bf16[4,4,4,4,16,1024]{5,4,3,2,1,0:T(8,128)(2,1)}, bf16[4,4,4,16,1024]{4,3,2,1,0:T(8,128)(2,1)}) custom-call(bf16[1024,1024]{1,0:T(8,128)(2,1)} %get-tuple-element.42.refs_0_.x_ref, bf16[4096,1024]{1,0:T(8,128)(2,1)} %bitcast.20, ...), custom_call_target="tpu_custom_call" | custom-call | flops 17179869184 | bytes 41943040 | tf_op jit(solution)/shard_map/forward_layer/pallas_call | solution.py:463
  109.6 32.1 %forward_layer.4 = (bf16[1024,1024]{1,0:T(8,128)(2,1)}, bf16[1024,2048]{1,0:T(8,128)(2,1)}, f32[1024,2048]{1,0:T(8,128)}, bf16[4,4,4,4,16,1024]{5,4,3,2,1,0:T(8,128)(2,1)}) custom-call(bf16[1024,1024]{1,0:T(8,128)(2,1)} %get-tuple-element.46.refs_0_.x_ref, bf16[4096,1024]{1,0:T(8,128)(2,1)} %bitcast.24, bf16[4,4,4,16,1024]{4,3,2,1,0:T(8,128)(2,1)} %get-tuple-element.48.refs_2_), custom_call_target="tpu_custom_call" | custom-call | flops 17179869184 | bytes 41943040 | tf_op jit(solution)/shard_map/forward_layer/pallas_call | solution.py:463
  141.7 40.3 %forward_layer.5 = (bf16[512,1024]{1,0:T(8,128)(2,1)}, bf16[1024,2048]{1,0:T(8,128)(2,1)}, f32[1024,2048]{1,0:T(8,128)}, bf16[4,4,4,4,16,1024]{5,4,3,2,1,0:T(8,128)(2,1)}) custom-call(bf16[1024,1024]{1,0:T(8,128)(2,1)} %get-tuple-element.49.refs_0_.x_ref, bf16[4096,1024]{1,0:T(8,128)(2,1)} %bitcast.25, bf16[4,4,16,1024]{3,2,1,0:T(8,128)(2,1)} %get-tuple-element.45.refs_3_.refs_2_), custom_call_target="tpu_custom_call" | custom-call | flops 17179869184 | bytes 41943040 | tf_op jit(solution)/shard_map/forward_layer/pallas_call | solution.py:463
  182.0 45.3 %backward_layer.3 = (bf16[1024,1024]{1,0:T(8,128)(2,1)}, bf16[1024,2048]{1,0:T(8,128)(2,1)}, f32[4,4,4,16,1024]{4,3,2,1,0:T(8,128)}, bf16[4,4,4,4,16,1024]{5,4,3,2,1,0:T(8,128)(2,1)}, bf16[4,4,16,1024]{3,2,1,0:T(8,128)(2,1)}) custom-call(bf16[1024,1024]{1,0:T(8,128)(2,1)} %get-tuple-element.52.refs_0_.g_ref, bf16[4096,1024]{1,0:T(8,128)(2,1)} %bitcast.23, ...), custom_call_target="tpu_custom_call" | custom-call | flops 17179869184 | bytes 41943040 | tf_op jit(solution)/shard_map/backward_layer/pallas_call | solution.py:463
  227.3 76.7 %scatter_sum.5 = (f32[8,4096]{1,0:T(8,128)}, f32[32,1024]{1,0:T(8,128)}) custom-call(bf16[1024,1024]{1,0:T(8,128)(2,1)} %get-tuple-element.49.refs_0_.x_ref, bf16[1024,2048]{1,0:T(8,128)(2,1)} %get-tuple-element.55.refs_3_.act_ref, bf16[1024,2048]{1,0:T(8,128)(2,1)} %get-tuple-element.74.d_pre_ref, bf16[1024,1024]{1,0:T(8,128)(2,1)} %get-tuple-element.52.refs_0_.g_ref, ...), custom_call_target="tpu_custom_call" | custom-call | flops 8589934592 | bytes 12582912 | tf_op jit(solution)/shard_map/scatter_sum/pallas_call | solution.py:638
  303.9 46.6 %backward_layer.4 = (bf16[1024,1024]{1,0:T(8,128)(2,1)}, bf16[1024,2048]{1,0:T(8,128)(2,1)}, f32[4,4,4,16,1024]{4,3,2,1,0:T(8,128)}, bf16[4,4,4,4,16,1024]{5,4,3,2,1,0:T(8,128)(2,1)}) custom-call(bf16[1024,1024]{1,0:T(8,128)(2,1)} %get-tuple-element.58.refs_0_.g_ref, bf16[4096,1024]{1,0:T(8,128)(2,1)} %bitcast.21, f32[1024,2048]{1,0:T(8,128)} %get-tuple-element.60.refs_2_, ...), custom_call_target="tpu_custom_call" | custom-call | flops 17179869184 | bytes 41943040 | tf_op jit(solution)/shard_map/backward_layer/pallas_call | solution.py:463
  350.5 76.3 %scatter_sum.4 = (f32[8,4096]{1,0:T(8,128)}, f32[32,1024]{1,0:T(8,128)}) custom-call(bf16[1024,1024]{1,0:T(8,128)(2,1)} %get-tuple-element.46.refs_0_.x_ref, bf16[1024,2048]{1,0:T(8,128)(2,1)} %get-tuple-element.61.refs_3_.act_ref, bf16[1024,2048]{1,0:T(8,128)(2,1)} %get-tuple-element.71.d_pre_ref, bf16[1024,1024]{1,0:T(8,128)(2,1)} %get-tuple-element.58.refs_0_.g_ref, ...), custom_call_target="tpu_custom_call" | custom-call | flops 8589934592 | bytes 12582912 | tf_op jit(solution)/shard_map/scatter_sum/pallas_call | solution.py:638
  426.8 22.9 %backward_layer.5 = (bf16[512,1024]{1,0:T(8,128)(2,1)}, bf16[1024,2048]{1,0:T(8,128)(2,1)}, f32[4,4,4,16,1024]{4,3,2,1,0:T(8,128)}) custom-call(bf16[1024,1024]{1,0:T(8,128)(2,1)} %get-tuple-element.63.refs_0_.g_ref, bf16[4096,1024]{1,0:T(8,128)(2,1)} %bitcast.22, f32[1024,2048]{1,0:T(8,128)} %get-tuple-element.65.refs_2_, ...), custom_call_target="tpu_custom_call" | custom-call | flops 17179869184 | bytes 41943040 | tf_op jit(solution)/shard_map/backward_layer/pallas_call | solution.py:463
  449.8 0.0 copy-start.2
  449.8 0.0 copy-start.4
  449.8 0.0 copy-start.1
  449.8 0.0 copy-start.3
  449.8 77.4 %scatter_sum.3 = (f32[8,4096]{1,0:T(8,128)}, f32[32,1024]{1,0:T(8,128)}) custom-call(bf16[1024,1024]{1,0:T(8,128)(2,1)} %get-tuple-element.42.refs_0_.x_ref, bf16[1024,2048]{1,0:T(8,128)(2,1)} %get-tuple-element.66.refs_3_.act_ref, bf16[1024,2048]{1,0:T(8,128)(2,1)} %get-tuple-element.68.d_pre_ref, bf16[1024,1024]{1,0:T(8,128)(2,1)} %get-tuple-element.63.refs_0_.g_ref, ...), custom_call_target="tpu_custom_call" | custom-call | flops 8589934592 | bytes 12582912 | tf_op jit(solution)/shard_map/scatter_sum/pallas_call | solution.py:638
  527.2 0.0 copy-start
  527.3 0.0 copy-done.2
  527.3 0.0 copy-done.4
  527.3 1.8 pad_maximum_fusion
  529.0 0.0 copy-done.1
  529.0 0.0 copy-done.3
  529.0 1.7 pad_maximum_fusion.1
  530.7 2.3 copy.10
  533.0 0.0 copy-done
  533.0 1.0 copy.11
Async XLA Ops:
  449.8 77.5 %copy-start.2 = (f32[8,4096]{1,0:T(8,128)S(1)}, f32[8,4096]{1,0:T(8,128)}, u32[]{:S(2)}) copy-start(f32[8,4096]{1,0:T(8,128)} %get-tuple-element.76) | copy-start | bytes 393220
  449.8 77.5 %copy-start.4 = (f32[8,4096]{1,0:T(8,128)S(1)}, f32[8,4096]{1,0:T(8,128)}, u32[]{:S(2)}) copy-start(f32[8,4096]{1,0:T(8,128)} %get-tuple-element.73) | copy-start | bytes 393220
  449.8 79.2 %copy-start.1 = (f32[32,1024]{1,0:T(8,128)S(1)}, f32[32,1024]{1,0:T(8,128)}, u32[]{:S(2)}) copy-start(f32[32,1024]{1,0:T(8,128)} %get-tuple-element.79) | copy-start | bytes 393220
  449.8 79.2 %copy-start.3 = (f32[32,1024]{1,0:T(8,128)S(1)}, f32[32,1024]{1,0:T(8,128)}, u32[]{:S(2)}) copy-start(f32[32,1024]{1,0:T(8,128)} %get-tuple-element.78) | copy-start | bytes 393220
  527.2 5.7 %copy-start = (bf16[512,1024]{1,0:T(8,128)(2,1)S(1)}, bf16[512,1024]{1,0:T(8,128)(2,1)}, u32[]{:S(2)}) copy-start(bf16[512,1024]{1,0:T(8,128)(2,1)} %get-tuple-element.85) | copy-start | bytes 3145732

commit v5 on v4

--- a/solution.py
+++ b/solution.py
@@ -1,4 +1,5 @@
 import functools
+import itertools
 import math
 
 import jax
@@ -132,13 +133,8 @@
             for slot in ((1, 2) if phase == 0 else (2, 3, 4, 5)):
                 self.net.got((job, phase, slot))
 
-    def through(self, phase):
-        self.send(phase)
-        self.forward(phase)
-        self.finish(phase)
-
     def load(self, src, fixed, sems):
-        return [pltpu.make_async_copy(self.block(job, fixed, ref=src, skip=fixed, more=None), self.block(job, fixed), sems.at[job])
+        return [pltpu.make_async_copy(self.block(job, fixed, ref=src, skip=fixed), self.block(job, fixed), sems.at[job])
                 for job in JOBS]
 
     def store(self, out, d, sems):
@@ -311,10 +307,22 @@
     me, near = ring_places()
     core = lax.axis_index("c")
     partner = 1 - core
-    loads = [pltpu.make_async_copy(stream, cur, loc_sem.at[0]), pltpu.make_async_copy(weights, mats, loc_sem.at[1])]
+    first_rows, second_rows = (pl.ds(k * 2 * width, 2 * width) for k in ((0, 1) if forward else (1, 0)))
+    early = [pltpu.make_async_copy(stream, cur, loc_sem.at[0]),
+             pltpu.make_async_copy(weights.at[first_rows], mats.at[first_rows], loc_sem.at[1])]
+    second = pltpu.make_async_copy(weights.at[second_rows], mats.at[second_rows], loc_sem.at[2])
+
+    def tile_rows(tile):
+        return pl.ds(tile * TILE if isinstance(tile, int) else pl.multiple_of(tile * TILE, TILE), TILE)
+
+    def slope_load(tile):
+        rows = tile_rows(tile)
+        return pltpu.make_async_copy(slope_in.at[rows], slope.at[rows], loc_sem.at[4 + tile])
+
+    loads = early + [second]
     if not forward:
-        loads.append(pltpu.make_async_copy(slope_in, slope, loc_sem.at[2]))
-        loads.append(pltpu.make_async_copy(act_in.at[:, pl.ds(width, width)], act_low, loc_sem.at[3]))
+        low_load = pltpu.make_async_copy(act_in.at[:, pl.ds(width, width)], act_low, loc_sem.at[3])
+        loads = early + [slope_load(0), second, low_load] + [slope_load(tile) for tile in range(1, tiles)]
     firsts = []
     if source:
         buf, send_sem, recv_sem, start_sem, store_sem = refs[10:15]
@@ -340,10 +348,10 @@
     if pre:
         before.send(0)
     if source == "line":
-        ring.through(1)
-    if source:
+        ring.send(1)
+    elif source:
         ring.last_sends(next_out, store_sem)
-    for copy in loads:
+    for copy in early:
         copy.wait()
 
     def exchange(tile):
@@ -352,9 +360,11 @@
             src_ref=part.at[rows], dst_ref=got.at[rows], send_sem=pair_send.at[tile], recv_sem=pair_recv.at[tile],
             device_id={"c": partner}, device_id_type=MESH)
 
-    def compute(tile, _):
-        rows = pl.ds(pl.multiple_of(tile * TILE, TILE), TILE)
+    def compute(tile, late=None):
+        rows = tile_rows(tile)
         left = cur[rows, :]
+        if not forward:
+            slope_load(tile).wait()
         for block in range(2):
             for cut in range(width // WIDE):
                 cols = pl.ds(block * width + cut * WIDE, WIDE)
@@ -367,12 +377,20 @@
                     low = (2 + block) * width + cut * WIDE
                     d_act = dot_nt(left, mats[low:low + WIDE, :])
                     act[rows, cols] = (d_act * slope[rows, cols]).astype(BF16)
+        if late is not None:
+            late.wait()
         if forward:
             part[rows, :] = dot_nn(act[rows, :], mats[2 * width:, :])
         else:
             part[rows, :] = dot_nt(act[rows, :width], mats[:width, :]) + dot_nt(act[rows, width:], mats[width:2 * width, :])
         exchange(tile).start()
-        return 0
+
+    def compute_tiles(low, high):
+        def step(tile, _):
+            compute(tile)
+            return 0
+
+        lax.fori_loop(low, high, step, 0)
 
     def low_slab(z, _):
         slab = width // SIDE
@@ -389,21 +407,33 @@
             saves.append(pltpu.make_async_copy(src.at[rows], dst.at[rows], out_sem.at[2 * k + n]))
             saves[-1].start()
 
-    mid = tiles // 2
-    lax.fori_loop(0, mid, compute, 0)
-    save(0, 0, mid)
-    if source:
+    head = tiles // 2 if source == "quarter" else 1
+    if head == 1:
+        compute(0, second)
+    else:
+        second.wait()
+        compute_tiles(0, head)
+    save(0, 0, head)
+    if source == "quarter":
         ring.forward(2)
+    elif source:
+        ring.forward(1)
     if ahead:
         after.forward(1)
     if pre:
         before.forward(0)
     if not forward:
+        low_load.wait()
         lax.fori_loop(0, SIDE, low_slab, 0)
         saves.append(pltpu.make_async_copy(grad_low, grad_out, out_sem.at[1]))
         saves[-1].start()
-    lax.fori_loop(mid, tiles, compute, 0)
-    save(1, mid, tiles)
+    if source == "line":
+        ring.finish(1)
+        ring.last_sends(next_out, store_sem)
+    compute_tiles(head, tiles)
+    save(1, head, tiles)
+    if source == "line":
+        ring.forward(2)
     for tile in range(tiles):
         exchange(tile).wait_recv()
 
@@ -451,7 +481,7 @@
     scratch = [pltpu.VMEM((tokens, width), BF16), pltpu.VMEM((4 * width, width), BF16),
                pltpu.VMEM((tokens, hidden), BF16), pltpu.VMEM((tokens, hidden), F32),
                pltpu.VMEM((tokens, width), F32), pltpu.VMEM((tokens, width), F32),
-               sems((tiles,)), sems((tiles,)), sems((4,)), sems((5,))]
+               sems((tiles,)), sems((tiles,)), sems((4 + tiles,)), sems((5,))]
     if source:
         scratch += [pltpu.VMEM(whole, BF16)] + RING_SEMS + [sems((6,)), sems((6, 4))]
     if ahead is not None:
@@ -467,7 +497,6 @@
         out_specs=[pl.BlockSpec(memory_space=pltpu.VMEM)] + [pl.BlockSpec(memory_space=pl.ANY)] * (len(outs) - 1),
         scratch_shapes=scratch,
         compiler_params=pltpu.CompilerParams(collective_id=call_id, has_side_effects=True, vmem_limit_bytes=VMEM_LIMIT),
-        cost_estimate=pl.CostEstimate(flops=8 * tokens * hidden * width, bytes_accessed=40 << 20, transcendentals=0),
         name="forward_layer" if forward else "backward_layer",
     )(*args)
 
@@ -646,7 +675,6 @@
         + RING_SEMS + [pltpu.SemaphoreType.DMA((5,)), pltpu.VMEM((2, 8, width), F32), pltpu.VMEM((8 * (width // 128), 512), F32),
                        pltpu.SemaphoreType.DMA((2,)), pltpu.SemaphoreType.DMA((2,)), pltpu.SemaphoreType.DMA((3, 4))],
         compiler_params=pltpu.CompilerParams(collective_id=call_id, has_side_effects=True, vmem_limit_bytes=VMEM_LIMIT),
-        cost_estimate=pl.CostEstimate(flops=8 * tokens * width * width, bytes_accessed=12 << 20, transcendentals=0),
         name="scatter_sum",
     )(x_in, act, d_pre, g_in, low)
 
@@ -657,16 +685,17 @@
     weight_spec = P(None, ALL, None)
 
     def device_step(x_loc, up_loc, down_loc, g_loc):
-        x_0, g_3, packed, full, quarter_1, line_1, line_2 = open_call(up_loc, down_loc, x_loc, g_loc, 0)
-        x_1, act_0, slope_0, full, quarter_2 = layer_call(True, x_0, full, None, 1, "quarter", quarter_1, line_2)
-        x_2, act_1, slope_1, full = layer_call(True, x_1, full, None, 2, "quarter", quarter_2)
-        y_out, act_2, slope_2, full = layer_call(True, x_2, full, None, 3, "line", line_2, last_layer=True)
-        g_2, d_pre_2, low_2, full, line_0 = layer_call(False, g_3, full, (slope_2, act_2), 4, "line", line_1, pre=packed)
-        sum_2 = scatter_sum(x_2, act_2, d_pre_2, g_3, low_2, 5)
-        g_1, d_pre_1, low_1, full = layer_call(False, g_2, full, (slope_1, act_1), 6, "line", line_0)
-        sum_1 = scatter_sum(x_1, act_1, d_pre_1, g_2, low_1, 7)
-        grad_in, d_pre_0, low_0 = layer_call(False, g_1, full, (slope_0, act_0), 8, last_layer=True)
-        sum_0 = scatter_sum(x_0, act_0, d_pre_0, g_1, low_0, 9)
+        ids = itertools.count()
+        x_0, g_3, packed, full, quarter_1, line_1, line_2 = open_call(up_loc, down_loc, x_loc, g_loc, next(ids))
+        x_1, act_0, slope_0, full, quarter_2 = layer_call(True, x_0, full, None, next(ids), "quarter", quarter_1, line_2)
+        x_2, act_1, slope_1, full = layer_call(True, x_1, full, None, next(ids), "quarter", quarter_2)
+        y_out, act_2, slope_2, full = layer_call(True, x_2, full, None, next(ids), "line", line_2, last_layer=True)
+        g_2, d_pre_2, low_2, full, line_0 = layer_call(False, g_3, full, (slope_2, act_2), next(ids), "line", line_1, pre=packed)
+        sum_2 = scatter_sum(x_2, act_2, d_pre_2, g_3, low_2, next(ids))
+        g_1, d_pre_1, low_1, full = layer_call(False, g_2, full, (slope_1, act_1), next(ids), "line", line_0)
+        sum_1 = scatter_sum(x_1, act_1, d_pre_1, g_2, low_1, next(ids))
+        grad_in, d_pre_0, low_0 = layer_call(False, g_1, full, (slope_0, act_0), next(ids), last_layer=True)
+        sum_0 = scatter_sum(x_0, act_0, d_pre_0, g_1, low_0, next(ids))
         grad_up, grad_down = (jnp.stack(parts) for parts in zip(sum_0, sum_1, sum_2, strict=True))
         return y_out, grad_in, grad_up, grad_down
 

time: 543 us -> 539 us (level)
    pallas_call x6, Pallas kernels: 227 us -> 220 us  [layer_call(): pl.pallas_call(functools.partial(layer_kernel, forward, width, source, ah...]
where the time goes in v5:
time: 539 us; the launch traced here: 531 us
  Pallas kernels  523 us (97%)
    pallas_call x3, Pallas kernels, scatter_sum(): pl.pallas_call(functools.partial(sum_kernel, width), out_shape=[jax.Shape...  234 us
    pallas_call x6, Pallas kernels, layer_call(): pl.pallas_call(functools.partial(layer_kernel, forward, width, source, ah...  220 us
    pallas_call x1, Pallas kernels, open_call(): pl.pallas_call(functools.partial(open_kernel, width), out_shape=[shape(2...  69.5 us

profile of v5, /device:TPU:1, one launch (start us, length us, event | category | flops | bytes accessed | tf_op | source)
XLA Modules:
  0.0 530.9 jit_solution(4933220385262638295)
XLA Ops:
  0.6 69.5 %open.1 = (bf16[1024,1024]{1,0:T(8,128)(2,1)}, bf16[1024,1024]{1,0:T(8,128)(2,1)}, bf16[4,16,1024]{2,1,0:T(8,128)(2,1)}, bf16[4,4,4,4,16,1024]{5,4,3,2,1,0:T(8,1...) custom-call(bf16[3,8,4096]{2,1,0:T(8,128)(2,1)} %up.1, ...), custom_call_target="tpu_custom_call" | custom-call | tf_op jit(solution)/shard_map/open/pallas_call | solution.py:271
  70.2 39.4 %forward_layer.3 = (bf16[1024,1024]{1,0:T(8,128)(2,1)}, bf16[1024,2048]{1,0:T(8,128)(2,1)}, f32[1024,2048]{1,0:T(8,128)}, bf16[4,4,4,4,16,1024]{5,4,3,2,1,0:T(8,128)(2,1)}, bf16[4,4,4,16,1024]{4,3,2,1,0:T(8,128)(2,1)}) custom-call(bf16[1024,1024]{1,0:T(8,128)(2,1)} %get-tuple-element.42.refs_0_.x_ref, bf16[4096,1024]{1,0:T(8,128)(2,1)} %bitcast.16, ...), custom_call_target="tpu_custom_call" | custom-call | tf_op jit(solution)/shard_map/forward_layer/pallas_call | solution.py:493
  109.6 33.3 %forward_layer.4 = (bf16[1024,1024]{1,0:T(8,128)(2,1)}, bf16[1024,2048]{1,0:T(8,128)(2,1)}, f32[1024,2048]{1,0:T(8,128)}, bf16[4,4,4,4,16,1024]{5,4,3,2,1,0:T(8,128)(2,1)}) custom-call(bf16[1024,1024]{1,0:T(8,128)(2,1)} %get-tuple-element.46.refs_0_.x_ref, bf16[4096,1024]{1,0:T(8,128)(2,1)} %bitcast.15, bf16[4,4,4,16,1024]{4,3,2,1,0:T(8,128)(2,1)} %get-tuple-element.48.refs_2_), custom_call_target="tpu_custom_call" | custom-call | tf_op jit(solution)/shard_map/forward_layer/pallas_call | solution.py:493
  142.9 38.5 %forward_layer.5 = (bf16[512,1024]{1,0:T(8,128)(2,1)}, bf16[1024,2048]{1,0:T(8,128)(2,1)}, f32[1024,2048]{1,0:T(8,128)}, bf16[4,4,4,4,16,1024]{5,4,3,2,1,0:T(8,128)(2,1)}) custom-call(bf16[1024,1024]{1,0:T(8,128)(2,1)} %get-tuple-element.49.refs_0_.x_ref, bf16[4096,1024]{1,0:T(8,128)(2,1)} %bitcast.17, bf16[4,4,16,1024]{3,2,1,0:T(8,128)(2,1)} %get-tuple-element.45.refs_3_.refs_2_), custom_call_target="tpu_custom_call" | custom-call | tf_op jit(solution)/shard_map/forward_layer/pallas_call | solution.py:493
  181.4 43.2 %backward_layer.3 = (bf16[1024,1024]{1,0:T(8,128)(2,1)}, bf16[1024,2048]{1,0:T(8,128)(2,1)}, f32[4,4,4,16,1024]{4,3,2,1,0:T(8,128)}, bf16[4,4,4,4,16,1024]{5,4,3,2,1,0:T(8,128)(2,1)}, bf16[4,4,16,1024]{3,2,1,0:T(8,128)(2,1)}) custom-call(bf16[1024,1024]{1,0:T(8,128)(2,1)} %get-tuple-element.52.refs_0_.g_ref, bf16[4096,1024]{1,0:T(8,128)(2,1)} %bitcast.14, ...), custom_call_target="tpu_custom_call" | custom-call | tf_op jit(solution)/shard_map/backward_layer/pallas_call | solution.py:493
  224.6 79.6 %scatter_sum.5 = (f32[8,4096]{1,0:T(8,128)}, f32[32,1024]{1,0:T(8,128)}) custom-call(bf16[1024,1024]{1,0:T(8,128)(2,1)} %get-tuple-element.49.refs_0_.x_ref, bf16[1024,2048]{1,0:T(8,128)(2,1)} %get-tuple-element.55.refs_3_.act_ref, bf16[1024,2048]{1,0:T(8,128)(2,1)} %get-tuple-element.74.d_pre_ref, bf16[1024,1024]{1,0:T(8,128)(2,1)} %get-tuple-element.52.refs_0_.g_ref, ...), custom_call_target="tpu_custom_call" | custom-call | tf_op jit(solution)/shard_map/scatter_sum/pallas_call | solution.py:667
  304.2 45.4 %backward_layer.4 = (bf16[1024,1024]{1,0:T(8,128)(2,1)}, bf16[1024,2048]{1,0:T(8,128)(2,1)}, f32[4,4,4,16,1024]{4,3,2,1,0:T(8,128)}, bf16[4,4,4,4,16,1024]{5,4,3,2,1,0:T(8,128)(2,1)}) custom-call(bf16[1024,1024]{1,0:T(8,128)(2,1)} %get-tuple-element.58.refs_0_.g_ref, bf16[4096,1024]{1,0:T(8,128)(2,1)} %bitcast.13, f32[1024,2048]{1,0:T(8,128)} %get-tuple-element.60.refs_2_, ...), custom_call_target="tpu_custom_call" | custom-call | tf_op jit(solution)/shard_map/backward_layer/pallas_call | solution.py:493
  349.6 77.5 %scatter_sum.4 = (f32[8,4096]{1,0:T(8,128)}, f32[32,1024]{1,0:T(8,128)}) custom-call(bf16[1024,1024]{1,0:T(8,128)(2,1)} %get-tuple-element.46.refs_0_.x_ref, bf16[1024,2048]{1,0:T(8,128)(2,1)} %get-tuple-element.61.refs_3_.act_ref, bf16[1024,2048]{1,0:T(8,128)(2,1)} %get-tuple-element.71.d_pre_ref, bf16[1024,1024]{1,0:T(8,128)(2,1)} %get-tuple-element.58.refs_0_.g_ref, ...), custom_call_target="tpu_custom_call" | custom-call | tf_op jit(solution)/shard_map/scatter_sum/pallas_call | solution.py:667
  427.1 19.7 %backward_layer.5 = (bf16[512,1024]{1,0:T(8,128)(2,1)}, bf16[1024,2048]{1,0:T(8,128)(2,1)}, f32[4,4,4,16,1024]{4,3,2,1,0:T(8,128)}) custom-call(bf16[1024,1024]{1,0:T(8,128)(2,1)} %get-tuple-element.63.refs_0_.g_ref, bf16[4096,1024]{1,0:T(8,128)(2,1)} %bitcast.18, f32[1024,2048]{1,0:T(8,128)} %get-tuple-element.65.refs_2_, ...), custom_call_target="tpu_custom_call" | custom-call | tf_op jit(solution)/shard_map/backward_layer/pallas_call | solution.py:493
  446.8 0.0 copy-start.2
  446.8 0.0 copy-start.4
  446.8 0.0 copy-start.1
  446.8 0.0 copy-start.3
  446.9 76.8 %scatter_sum.3 = (f32[8,4096]{1,0:T(8,128)}, f32[32,1024]{1,0:T(8,128)}) custom-call(bf16[1024,1024]{1,0:T(8,128)(2,1)} %get-tuple-element.42.refs_0_.x_ref, bf16[1024,2048]{1,0:T(8,128)(2,1)} %get-tuple-element.66.refs_3_.act_ref, bf16[1024,2048]{1,0:T(8,128)(2,1)} %get-tuple-element.68.d_pre_ref, bf16[1024,1024]{1,0:T(8,128)(2,1)} %get-tuple-element.63.refs_0_.g_ref, ...), custom_call_target="tpu_custom_call" | custom-call | tf_op jit(solution)/shard_map/scatter_sum/pallas_call | solution.py:667
  523.7 0.0 copy-start
  523.7 0.0 copy-done.2
  523.7 0.0 copy-done.4
  523.7 1.8 pad_maximum_fusion
  525.5 0.0 copy-done.1
  525.5 0.0 copy-done.3
  525.5 1.7 pad_maximum_fusion.1
  527.2 2.3 copy.10
  529.4 0.0 copy-done
  529.4 1.0 copy.11
Async XLA Ops:
  446.8 76.9 %copy-start.2 = (f32[8,4096]{1,0:T(8,128)S(1)}, f32[8,4096]{1,0:T(8,128)}, u32[]{:S(2)}) copy-start(f32[8,4096]{1,0:T(8,128)} %get-tuple-element.76) | copy-start | bytes 393220
  446.8 76.9 %copy-start.4 = (f32[8,4096]{1,0:T(8,128)S(1)}, f32[8,4096]{1,0:T(8,128)}, u32[]{:S(2)}) copy-start(f32[8,4096]{1,0:T(8,128)} %get-tuple-element.73) | copy-start | bytes 393220
  446.8 78.7 %copy-start.1 = (f32[32,1024]{1,0:T(8,128)S(1)}, f32[32,1024]{1,0:T(8,128)}, u32[]{:S(2)}) copy-start(f32[32,1024]{1,0:T(8,128)} %get-tuple-element.79) | copy-start | bytes 393220
  446.8 78.7 %copy-start.3 = (f32[32,1024]{1,0:T(8,128)S(1)}, f32[32,1024]{1,0:T(8,128)}, u32[]{:S(2)}) copy-start(f32[32,1024]{1,0:T(8,128)} %get-tuple-element.78) | copy-start | bytes 393220
  523.7 5.7 %copy-start = (bf16[512,1024]{1,0:T(8,128)(2,1)S(1)}, bf16[512,1024]{1,0:T(8,128)(2,1)}, u32[]{:S(2)}) copy-start(bf16[512,1024]{1,0:T(8,128)(2,1)} %get-tuple-element.85) | copy-start | bytes 3145732

commit v6 on v5

--- a/solution.py
+++ b/solution.py
@@ -619,22 +619,22 @@
         ring.mid(job, 0)
     for job in SMALL:
         low[job, HERE].wait()
-    for phase in range(3):
-        for group in (SMALL, LARGE):
-            for job in group:
-                ring.finish(job, phase)
-                if phase < 2:
-                    ring.send(job, phase + 1)
-        if phase < 2:
-            for group in (SMALL, LARGE):
-                for job in group:
-                    ring.mid(job, phase + 1)
+    for phase in range(2):
+        for job in JOBS:
+            ring.finish(job, phase)
+            ring.send(job, phase + 1)
+        for job in JOBS:
+            ring.mid(job, phase + 1)
+    for job in LARGE[:2]:
+        ring.finish(job, 2)
     own = [view(buf, (mat,), CHIPS, me) for mat in range(4)]
     pair = [pltpu.make_async_remote_copy(
         src_ref=own[mat].at[pl.ds(pl.multiple_of(8 * (1 - core), 8), 8)], dst_ref=theirs.at[mat], send_sem=pair_send.at[mat],
         recv_sem=pair_recv.at[mat], device_id={"c": 1 - core}, device_id_type=MESH) for mat in range(2)]
     for copy in pair:
         copy.start()
+    for job in (LARGE[2], *SMALL):
+        ring.finish(job, 2)
     for mat in (2, 3):
         down_out[(mat - 2) * ROWS:(mat - 1) * ROWS, :] = own[mat][...]
     places = column_places(512, 512)
@@ -648,7 +648,7 @@
             rows, cols = slice(8 * group, 8 * group + 8), slice(128 * group, 128 * group + 128)
             wide[rows, 128 * mat:128 * mat + 128] = low[:, cols]
             wide[rows, 256 + 128 * mat:384 + 128 * mat] = high[:, cols]
-    rest_val = wide[...]
+    rest_val = wide[...] * 0.5
     total = None
     for _ in range(3):
         piece = rest_val.astype(BF16)
@@ -656,7 +656,7 @@
         term = dot_nt(piece, places)
         total = term if total is None else total + term
     for group in range(width // 128):
-        up_out[:, 512 * group:512 * group + 512] = total[8 * group:8 * group + 8, :]
+        up_out[:, 512 * group:512 * group + 512] = total[8 * group:8 * group + 8, :] * 2.0
     for copy in pair:
         copy.wait_send()
     ring.net.close()

time: 539 us -> 537 us (level)
  no operation moved by 1% of the time
where the time goes in v6:
time: 537 us; the launch traced here: 529 us
  Pallas kernels  521 us (97%)
    pallas_call x3, Pallas kernels, scatter_sum(): pl.pallas_call(functools.partial(sum_kernel, width), out_shape=[jax.Shape...  231 us
    pallas_call x6, Pallas kernels, layer_call(): pl.pallas_call(functools.partial(layer_kernel, forward, width, source, ah...  221 us
    pallas_call x1, Pallas kernels, open_call(): pl.pallas_call(functools.partial(open_kernel, width), out_shape=[shape(2...  69.5 us

profile of v6, /device:TPU:1, one launch (start us, length us, event | category | flops | bytes accessed | tf_op | source)
XLA Modules:
  0.0 529.4 jit_solution(9412792083377990476)
XLA Ops:
  0.6 69.5 %open.1 = (bf16[1024,1024]{1,0:T(8,128)(2,1)}, bf16[1024,1024]{1,0:T(8,128)(2,1)}, bf16[4,16,1024]{2,1,0:T(8,128)(2,1)}, bf16[4,4,4,4,16,1024]{5,4,3,2,1,0:T(8,1...) custom-call(bf16[3,8,4096]{2,1,0:T(8,128)(2,1)} %up.1, ...), custom_call_target="tpu_custom_call" | custom-call | tf_op jit(solution)/shard_map/open/pallas_call | solution.py:271
  70.2 39.4 %forward_layer.3 = (bf16[1024,1024]{1,0:T(8,128)(2,1)}, bf16[1024,2048]{1,0:T(8,128)(2,1)}, f32[1024,2048]{1,0:T(8,128)}, bf16[4,4,4,4,16,1024]{5,4,3,2,1,0:T(8,128)(2,1)}, bf16[4,4,4,16,1024]{4,3,2,1,0:T(8,128)(2,1)}) custom-call(bf16[1024,1024]{1,0:T(8,128)(2,1)} %get-tuple-element.42.refs_0_.x_ref, bf16[4096,1024]{1,0:T(8,128)(2,1)} %bitcast.16, ...), custom_call_target="tpu_custom_call" | custom-call | tf_op jit(solution)/shard_map/forward_layer/pallas_call | solution.py:493
  109.6 33.3 %forward_layer.4 = (bf16[1024,1024]{1,0:T(8,128)(2,1)}, bf16[1024,2048]{1,0:T(8,128)(2,1)}, f32[1024,2048]{1,0:T(8,128)}, bf16[4,4,4,4,16,1024]{5,4,3,2,1,0:T(8,128)(2,1)}) custom-call(bf16[1024,1024]{1,0:T(8,128)(2,1)} %get-tuple-element.46.refs_0_.x_ref, bf16[4096,1024]{1,0:T(8,128)(2,1)} %bitcast.15, bf16[4,4,4,16,1024]{4,3,2,1,0:T(8,128)(2,1)} %get-tuple-element.48.refs_2_), custom_call_target="tpu_custom_call" | custom-call | tf_op jit(solution)/shard_map/forward_layer/pallas_call | solution.py:493
  142.9 38.5 %forward_layer.5 = (bf16[512,1024]{1,0:T(8,128)(2,1)}, bf16[1024,2048]{1,0:T(8,128)(2,1)}, f32[1024,2048]{1,0:T(8,128)}, bf16[4,4,4,4,16,1024]{5,4,3,2,1,0:T(8,128)(2,1)}) custom-call(bf16[1024,1024]{1,0:T(8,128)(2,1)} %get-tuple-element.49.refs_0_.x_ref, bf16[4096,1024]{1,0:T(8,128)(2,1)} %bitcast.17, bf16[4,4,16,1024]{3,2,1,0:T(8,128)(2,1)} %get-tuple-element.45.refs_3_.refs_2_), custom_call_target="tpu_custom_call" | custom-call | tf_op jit(solution)/shard_map/forward_layer/pallas_call | solution.py:493
  181.4 43.2 %backward_layer.3 = (bf16[1024,1024]{1,0:T(8,128)(2,1)}, bf16[1024,2048]{1,0:T(8,128)(2,1)}, f32[4,4,4,16,1024]{4,3,2,1,0:T(8,128)}, bf16[4,4,4,4,16,1024]{5,4,3,2,1,0:T(8,128)(2,1)}, bf16[4,4,16,1024]{3,2,1,0:T(8,128)(2,1)}) custom-call(bf16[1024,1024]{1,0:T(8,128)(2,1)} %get-tuple-element.52.refs_0_.g_ref, bf16[4096,1024]{1,0:T(8,128)(2,1)} %bitcast.14, ...), custom_call_target="tpu_custom_call" | custom-call | tf_op jit(solution)/shard_map/backward_layer/pallas_call | solution.py:493
  224.6 77.6 %scatter_sum.5 = (f32[8,4096]{1,0:T(8,128)}, f32[32,1024]{1,0:T(8,128)}) custom-call(bf16[1024,1024]{1,0:T(8,128)(2,1)} %get-tuple-element.49.refs_0_.x_ref, bf16[1024,2048]{1,0:T(8,128)(2,1)} %get-tuple-element.55.refs_3_.act_ref, bf16[1024,2048]{1,0:T(8,128)(2,1)} %get-tuple-element.74.d_pre_ref, bf16[1024,1024]{1,0:T(8,128)(2,1)} %get-tuple-element.52.refs_0_.g_ref, ...), custom_call_target="tpu_custom_call" | custom-call | tf_op jit(solution)/shard_map/scatter_sum/pallas_call | solution.py:667
  302.3 46.5 %backward_layer.4 = (bf16[1024,1024]{1,0:T(8,128)(2,1)}, bf16[1024,2048]{1,0:T(8,128)(2,1)}, f32[4,4,4,16,1024]{4,3,2,1,0:T(8,128)}, bf16[4,4,4,4,16,1024]{5,4,3,2,1,0:T(8,128)(2,1)}) custom-call(bf16[1024,1024]{1,0:T(8,128)(2,1)} %get-tuple-element.58.refs_0_.g_ref, bf16[4096,1024]{1,0:T(8,128)(2,1)} %bitcast.13, f32[1024,2048]{1,0:T(8,128)} %get-tuple-element.60.refs_2_, ...), custom_call_target="tpu_custom_call" | custom-call | tf_op jit(solution)/shard_map/backward_layer/pallas_call | solution.py:493
  348.8 77.1 %scatter_sum.4 = (f32[8,4096]{1,0:T(8,128)}, f32[32,1024]{1,0:T(8,128)}) custom-call(bf16[1024,1024]{1,0:T(8,128)(2,1)} %get-tuple-element.46.refs_0_.x_ref, bf16[1024,2048]{1,0:T(8,128)(2,1)} %get-tuple-element.61.refs_3_.act_ref, bf16[1024,2048]{1,0:T(8,128)(2,1)} %get-tuple-element.71.d_pre_ref, bf16[1024,1024]{1,0:T(8,128)(2,1)} %get-tuple-element.58.refs_0_.g_ref, ...), custom_call_target="tpu_custom_call" | custom-call | tf_op jit(solution)/shard_map/scatter_sum/pallas_call | solution.py:667
  426.0 19.7 %backward_layer.5 = (bf16[512,1024]{1,0:T(8,128)(2,1)}, bf16[1024,2048]{1,0:T(8,128)(2,1)}, f32[4,4,4,16,1024]{4,3,2,1,0:T(8,128)}) custom-call(bf16[1024,1024]{1,0:T(8,128)(2,1)} %get-tuple-element.63.refs_0_.g_ref, bf16[4096,1024]{1,0:T(8,128)(2,1)} %bitcast.18, f32[1024,2048]{1,0:T(8,128)} %get-tuple-element.65.refs_2_, ...), custom_call_target="tpu_custom_call" | custom-call | tf_op jit(solution)/shard_map/backward_layer/pallas_call | solution.py:493
  445.7 0.0 copy-start.2
  445.7 0.0 copy-start.4
  445.7 0.0 copy-start.1
  445.7 0.0 copy-start.3
  445.7 76.5 %scatter_sum.3 = (f32[8,4096]{1,0:T(8,128)}, f32[32,1024]{1,0:T(8,128)}) custom-call(bf16[1024,1024]{1,0:T(8,128)(2,1)} %get-tuple-element.42.refs_0_.x_ref, bf16[1024,2048]{1,0:T(8,128)(2,1)} %get-tuple-element.66.refs_3_.act_ref, bf16[1024,2048]{1,0:T(8,128)(2,1)} %get-tuple-element.68.d_pre_ref, bf16[1024,1024]{1,0:T(8,128)(2,1)} %get-tuple-element.63.refs_0_.g_ref, ...), custom_call_target="tpu_custom_call" | custom-call | tf_op jit(solution)/shard_map/scatter_sum/pallas_call | solution.py:667
  522.2 0.0 copy-start
  522.2 0.0 copy-done.2
  522.2 0.0 copy-done.4
  522.3 1.8 pad_maximum_fusion
  524.0 0.0 copy-done.1
  524.0 0.0 copy-done.3
  524.0 1.7 pad_maximum_fusion.1
  525.7 2.3 copy.10
  528.0 0.0 copy-done
  528.0 1.0 copy.11
Async XLA Ops:
  445.7 76.6 %copy-start.2 = (f32[8,4096]{1,0:T(8,128)S(1)}, f32[8,4096]{1,0:T(8,128)}, u32[]{:S(2)}) copy-start(f32[8,4096]{1,0:T(8,128)} %get-tuple-element.76) | copy-start | bytes 393220
  445.7 76.6 %copy-start.4 = (f32[8,4096]{1,0:T(8,128)S(1)}, f32[8,4096]{1,0:T(8,128)}, u32[]{:S(2)}) copy-start(f32[8,4096]{1,0:T(8,128)} %get-tuple-element.73) | copy-start | bytes 393220
  445.7 78.3 %copy-start.1 = (f32[32,1024]{1,0:T(8,128)S(1)}, f32[32,1024]{1,0:T(8,128)}, u32[]{:S(2)}) copy-start(f32[32,1024]{1,0:T(8,128)} %get-tuple-element.79) | copy-start | bytes 393220
  445.7 78.3 %copy-start.3 = (f32[32,1024]{1,0:T(8,128)S(1)}, f32[32,1024]{1,0:T(8,128)}, u32[]{:S(2)}) copy-start(f32[32,1024]{1,0:T(8,128)} %get-tuple-element.78) | copy-start | bytes 393220
  522.2 5.7 %copy-start = (bf16[512,1024]{1,0:T(8,128)(2,1)S(1)}, bf16[512,1024]{1,0:T(8,128)(2,1)}, u32[]{:S(2)}) copy-start(bf16[512,1024]{1,0:T(8,128)(2,1)} %get-tuple-element.85) | copy-start | bytes 3145732
